TPU v7x, 128 devices: a whole 4x4x4 slice. The times are simulated.
128 devices in a mesh: dp: 16 (over z, x), shard: 8 (over y, core).
Axes of the slice: x: 4, y: 4, z: 4, core: 2. Of those that a mesh axis runs over, the one named last changes fastest.
Arguments:
- tokens: bfloat16 [32768, 2048], P(('dp', 'shard')), may hold values from -24 to 24
- ctx_cotangent: bfloat16 [32768, 1024], P(('dp', 'shard')), may hold values from -0.59765625 to 0.59765625
- latent_cache: bfloat16 [2048, 128, 896], P('dp', 'shard'), may hold values from -300 to 300
- nbr_ids: int32 [512, 2], P(('dp', 'shard')), may hold values from 0 to 2047, as said below
- w_query: bfloat16 [2048, 1024], P('shard'), may hold values from -0.125 to 0.125
- w_key: bfloat16 [896, 1024], P('shard'), may hold values from -0.1875 to 0.1875
- w_value: bfloat16 [896, 1024], P('shard'), may hold values from -0.1875 to 0.1875
Outputs:
- context: bfloat16 [32768, 1024], P(('dp', 'shard'))
- grad_query: float32 [2048, 1024], P(('dp', 'shard'))
- grad_key: float32 [896, 1024], P(('dp', 'shard'))
- grad_value: float32 [896, 1024], P(('dp', 'shard'))
Inputs may be any that keep to these rules, and one draw needn't show every extreme that they name: Row r of latent_cache is owned by index r // 128 of dp. Within the 64 ids of one index of dp (its devices' nbr_ids in row-major order), at most 8 name rows of one owner, and in every draw one owner is named exactly 8 times by every index of dp. Ids may repeat.
All inputs are finite; a program needn't handle non-finite values.
Results may differ from a plain program's by a relative error of at most 0.0055.
The roundings to bfloat16 on the way count: a program that leaves them out, or rounds other values in their place, can miss the bound.
Values may be sent and summed in bfloat16 or wider, within the bound.
A program may use at most 128 MiB of HBM per device.

v0:
```python
import jax
import jax.numpy as jnp
from jax import lax
from jax.sharding import PartitionSpec as P

LAT = 896
HEADS = 8
HEAD_DIM = 128
SPAN = 64
NBR = 2
NT = 128
CH_DEV = 4
INNER = 1024


def copy_for_each(array, axis):
    count = lax.axis_size(axis)
    return lax.all_to_all(
        jnp.broadcast_to(array[None], (count, *array.shape)), axis, 0, 0, tiled=True
    )


def laid_out(parts, dim):
    parts = jnp.moveaxis(parts, 0, dim)
    dims = parts.shape
    return parts.reshape(*dims[:dim], dims[dim] * dims[dim + 1], *dims[dim + 2 :])


def collect(array, axis, dim):
    parts = copy_for_each(array, axis)
    return laid_out(parts, dim)


def sent_together(arrays, axis, dim, along):
    both = jnp.concatenate(arrays, axis=along)
    whole, at, gathered = (lax.all_gather(both, axis, axis=dim, tiled=True), 0, [])
    for a in arrays:
        gathered.append(lax.slice_in_dim(whole, at, at + a.shape[along], axis=along))
        at += a.shape[along]
    return tuple(gathered)


def side_by_side(arrays, axis, dim, along):
    widths = [a.shape[along] for a in arrays]
    both = jnp.concatenate(arrays, axis=along)
    whole = lax.psum_scatter(both, axis, scatter_dimension=dim, tiled=True)
    return tuple(jnp.split(whole, [sum(widths[:k]) for k in range(1, len(widths))], axis=along))


def body(tokens, ctx_cotangent, latent_cache, nbr_ids, w_query, w_key, w_value):
    softmax_scale = HEAD_DIM ** (-0.5)
    owner_count = lax.axis_size("dp")
    shard_count = lax.axis_size("shard")
    owner_rows = latent_cache.shape[0]
    slice_tokens = latent_cache.shape[1]
    requests = nbr_ids.reshape(-1)
    gathered = collect(requests, "shard", 0)
    slot_count = 2 * gathered.shape[0] // owner_count
    owner_of = gathered // owner_rows
    within_row = gathered % owner_rows
    onehot = (owner_of[:, None] == jnp.arange(owner_count, dtype=jnp.int32)[None, :]).astype(
        jnp.int32
    )
    earlier = jnp.cumsum(onehot, axis=0) - onehot
    position = jnp.sum(earlier * onehot, axis=1)
    slot_of = owner_of * slot_count + position
    outgoing = jnp.zeros((owner_count * slot_count,), jnp.int32).at[slot_of].set(within_row)
    outgoing = outgoing.reshape(owner_count, slot_count)
    asked_rows = lax.all_to_all(outgoing, "dp", split_axis=0, concat_axis=0, tiled=True)
    fetched = latent_cache[asked_rows.reshape(-1)]
    fetched = fetched.reshape(asked_rows.shape[0], asked_rows.shape[1], slice_tokens, LAT)
    replies = lax.all_to_all(fetched, "dp", split_axis=0, concat_axis=0, tiled=True)
    arrived = replies.reshape(owner_count * slot_count, slice_tokens, LAT)
    chosen = arrived[slot_of].reshape(shard_count, -1, slice_tokens, LAT)
    latents = lax.all_to_all(chosen, "shard", split_axis=0, concat_axis=2, tiled=True)
    latent_rows = latents.reshape(-1, LAT)
    pieces = sent_together((w_key, w_value), "shard", 0, 1)
    columns = latent_rows
    key_sum = jnp.dot(columns, pieces[0], preferred_element_type=jnp.float32)
    value_sum = jnp.dot(columns, pieces[1], preferred_element_type=jnp.float32)
    key_rows = key_sum.astype(jnp.bfloat16)
    value_rows = value_sum.astype(jnp.bfloat16)
    as_float = tokens.astype(jnp.float32)
    normed = (
        as_float * lax.rsqrt(jnp.mean(as_float * as_float, axis=-1, keepdims=True) + 1e-06)
    ).astype(jnp.bfloat16)
    columns = normed
    query_sum = jnp.dot(
        columns,
        lax.all_gather(w_query, "shard", axis=0, tiled=True),
        preferred_element_type=jnp.float32,
    )
    queries = (query_sum * softmax_scale).astype(jnp.bfloat16)
    query_heads = queries.reshape(CH_DEV, SPAN, HEADS, HEAD_DIM)
    key_heads = key_rows.reshape(CH_DEV, NBR * NT, HEADS, HEAD_DIM)
    value_heads = value_rows.reshape(CH_DEV, NBR * NT, HEADS, HEAD_DIM)
    scores = jnp.einsum(
        "cmhd,cnhd->chmn", query_heads, key_heads, preferred_element_type=jnp.float32
    )
    highest = jnp.max(scores, axis=-1, keepdims=True)
    exp_scores = jnp.exp(scores - highest)
    attn_prob = exp_scores / jnp.sum(exp_scores, axis=-1, keepdims=True)
    prob_round = attn_prob.astype(jnp.bfloat16)
    context = jnp.einsum(
        "chmn,cnhd->cmhd", prob_round, value_heads, preferred_element_type=jnp.float32
    ).astype(jnp.bfloat16)
    grad_heads = ctx_cotangent.reshape(CH_DEV, SPAN, HEADS, HEAD_DIM)
    value_grad = jnp.einsum(
        "chmn,cmhd->cnhd", prob_round, grad_heads, preferred_element_type=jnp.float32
    ).astype(jnp.bfloat16)
    prob_grad = jnp.einsum(
        "cmhd,cnhd->chmn", grad_heads, value_heads, preferred_element_type=jnp.float32
    )
    score_grad = attn_prob * (prob_grad - jnp.sum(attn_prob * prob_grad, axis=-1, keepdims=True))
    score_grad = score_grad.astype(jnp.bfloat16)
    query_grad = (
        jnp.einsum("chmn,cnhd->cmhd", score_grad, key_heads, preferred_element_type=jnp.float32)
        * softmax_scale
    ).astype(jnp.bfloat16)
    key_grad = jnp.einsum(
        "chmn,cmhd->cnhd", score_grad, query_heads, preferred_element_type=jnp.float32
    ).astype(jnp.bfloat16)
    query_grad = query_grad.reshape(-1, INNER)
    key_grad = key_grad.reshape(-1, INNER)
    value_grad = value_grad.reshape(-1, INNER)
    term_query = jnp.einsum("td,te->de", normed, query_grad, preferred_element_type=jnp.float32)
    term_key = jnp.einsum("tl,te->le", latent_rows, key_grad, preferred_element_type=jnp.float32)
    term_value = jnp.einsum(
        "tl,te->le", latent_rows, value_grad, preferred_element_type=jnp.float32
    )
    split_query = term_query.reshape(owner_count, shard_count, -1, INNER)
    split_key = term_key.reshape(owner_count, shard_count, -1, INNER)
    split_value = term_value.reshape(owner_count, shard_count, -1, INNER)
    inner_query, inner_key, inner_value = side_by_side(
        (split_query, split_key, split_value), "shard", 1, 2
    )
    outer_query, outer_key, outer_value = side_by_side(
        (inner_query, inner_key, inner_value), "dp", 0, 2
    )
    grad_query = outer_query.reshape(-1, INNER)
    grad_key = outer_key.reshape(-1, INNER)
    grad_value = outer_value.reshape(-1, INNER)
    return (context.reshape(-1, INNER), grad_query, grad_key, grad_value)


def solution(mesh):
    return jax.shard_map(
        body,
        mesh=mesh,
        in_specs=(
            P(("dp", "shard"), None),
            P(("dp", "shard"), None),
            P("dp", "shard", None),
            P(("dp", "shard"), None),
            P("shard", None),
            P("shard", None),
            P("shard", None),
        ),
        out_specs=(
            P(("dp", "shard"), None),
            P(("dp", "shard"), None),
            P(("dp", "shard"), None),
            P(("dp", "shard"), None),
        ),
        check_vma=False,
    )
```

profile of v0, /device:TPU:0, one launch (start us, length us, event | category | flops | bytes accessed | tf_op | source)
XLA Modules:
  0.0 408.3 jit_solution(17144313519049257396)
XLA Ops:
  10.7 9.7 %all_to_all.35 = s32[8,1,8]{2,1,0:T(1,128)S(1)} all-to-all(s32[8,1,8]{2,1,0:T(1,128)S(1)} %broadcast_in_dim.5), channel_id=1, replica_groups=mesh['dp'=16,'shard'=8] {'shard'}, dimensions={0} | all-to-all | bytes 512 | tf_op jit(solution)/shard_map/all_to_all | solution.py:18
  23.0 15.3 %all_to_all.36 = s32[16,1,8]{2,1,0:T(1,128)S(1)} all-to-all(s32[16,1,8]{2,1,0:T(1,128)S(1)} %bitcast.112), channel_id=1, replica_groups=mesh['dp'=16,'shard'=8] {'dp'}, dimensions={0} | all-to-all | bytes 1024 | tf_op jit(solution)/shard_map/all_to_all | solution.py:69
  39.0 4.9 %gather_fusion = bf16[128,16,896]{2,1,0:T(8,128)(2,1)} fusion(bf16[128,16,896]{2,1,0:T(8,128)(2,1)} %param.9, s32[1024]{0:T(1024)S(1)} %pad_clamp_fusion.1), kind=kCustom, calls=%fused_computation | custom fusion | bytes 7340544 | tf_op jit(solution)/shard_map/gather | solution.py:70
  43.9 4.5 %all-to-all-start.2 = ((bf16[16,8,16,896]{3,2,1,0:T(8,128)(2,1)}), bf16[16,8,16,896]{3,2,1,0:T(8,128)(2,1)}, u32[]{:S(2)}, u32[]{:S(2)}) async-start(bf16[16,8,16,896]{3,2,1,0:T(8,128)(2,1)} %bitcast.94), calls=%async_computation.2 | async-start | bytes 7340032 | tf_op jit(solution)/shard_map/all_to_all | solution.py:72
  48.5 52.0 %all-to-all-done.2 = bf16[16,8,16,896]{3,2,1,0:T(8,128)(2,1)} async-done(((bf16[16,8,16,896]{3,2,1,0:T(8,128)(2,1)}), bf16[16,8,16,896]{3,2,1,0:T(8,128)(2,1)}, u32[]{:S(2)}, u32[]{:S(2)}) %all-to-all-start.2) | async-done | bytes 3670048 | tf_op jit(solution)/shard_map/all_to_all | solution.py:72
  100.5 4.1 %gather_fusion.1 = bf16[64,16,896]{2,1,0:T(8,128)(2,1)} fusion(bf16[128,16,896]{2,1,0:T(8,128)(2,1)} %bitcast.5, s32[1024]{0:T(1024)S(1)} %pad_clamp_fusion), kind=kCustom, calls=%fused_computation.1 | custom fusion | bytes 3670272 | tf_op jit(solution)/shard_map/gather | solution.py:74
  104.6 4.4 %all-to-all-start.3 = ((bf16[8,8,16,896]{3,2,1,0:T(8,128)(2,1)}), bf16[8,8,16,896]{3,2,1,0:T(8,128)(2,1)}, u32[]{:S(2)}, u32[]{:S(2)}) async-start(bf16[8,8,16,896]{3,2,1,0:T(8,128)(2,1)} %bitcast.6), calls=%async_computation.3 | async-start | bytes 3670016 | tf_op jit(solution)/shard_map/all_to_all | solution.py:75
  111.3 22.2 %all-to-all-done.3 = bf16[8,8,16,896]{3,2,1,0:T(8,128)(2,1)} async-done(((bf16[8,8,16,896]{3,2,1,0:T(8,128)(2,1)}), bf16[8,8,16,896]{3,2,1,0:T(8,128)(2,1)}, u32[]{:S(2)}, u32[]{:S(2)}) %all-to-all-start.3) | async-done | bytes 1835040 | tf_op jit(solution)/shard_map/all_to_all | solution.py:75
  137.6 3.8 dot_general.58
  141.4 3.8 convert_bitcast_fusion.3
  152.4 3.6 fusion.36
  159.0 6.7 %convert_bitcast_fusion = bf16[4,256,8,128]{3,1,2,0:T(8,128)(2,1)} fusion(bf16[4,64,8,128]{3,2,1,0:T(8,128)(2,1)} %bitcast.107, f32[4,8,64]{2,1,0:T(8,128)S(1)} %get-tuple-element.8, f32[4,8,64,256]{3,2,1,0:T(8,128)S(1)} %fusion.16), kind=kOutput, calls=%fused_computation.18 | convolution fusion | flops 136841472 | bytes 4726784 | tf_op jit(solution)/shard_map/chmn,cmhd->cnhd/dot_general | solution.py:108
  165.7 3.5 fusion.7
  173.6 2.7 copy.79
  176.3 4.1 %reshape.265 = bf16[1024,1024,1,1]{1,0,2,3:T(8,128)(2,1)} reshape(bf16[4,256,8,128]{3,2,1,0:T(8,128)(2,1)} %copy.79) | data formatting | bytes 4194304 | tf_op jit(solution)/shard_map/reshape | solution.py:125
  183.0 4.3 %reshape.264 = bf16[1024,1024,1,1]{1,0,2,3:T(8,128)(2,1)} reshape(bf16[4,256,8,128]{3,2,1,0:T(8,128)(2,1)} %copy.76) | data formatting | bytes 4194304 | tf_op jit(solution)/shard_map/reshape | solution.py:124
  187.4 6.9 %fusion.3 = f32[16,8,7,1024]{3,2,1,0:T(8,128)} fusion(bf16[16,8,7,1024]{3,2,1,0:T(8,128)(2,1)} %dot_general.58, bf16[1024,1024,1,1]{1,0,2,3:T(8,128)(2,1)S(1)} %copy-done.10), kind=kOutput, calls=%fused_computation.9 | convolution fusion | flops 1879048192 | bytes 7602176 | tf_op jit(solution)/shard_map/tl,te->le/dot_general | solution.py:128
  194.3 5.3 %fusion.5 = f32[16,8,7,1024]{3,2,1,0:T(8,128)} fusion(bf16[16,8,7,1024]{3,2,1,0:T(8,128)(2,1)S(1)} %copy-done.12, bf16[1024,1024,1,1]{1,0,2,3:T(8,128)(2,1)S(1)} %copy-done.11), kind=kOutput, calls=%fused_computation.11 | convolution fusion | flops 1879048192 | bytes 7602176 | tf_op jit(solution)/shard_map/tl,te->le/dot_general | solution.py:127
  203.6 4.0 pad_maximum_fusion
  207.6 11.4 %copy.83 = f32[16,8,30,1024]{3,0,2,1:T(8,128)} copy(f32[16,8,30,1024]{3,2,1,0:T(8,128)S(1)} %pad_maximum_fusion) | data formatting | bytes 31457280 | tf_op jit(solution)/shard_map/concatenate | solution.py:45
  219.1 83.7 %reduce-scatter.2.cloned.1.call-done = f32[16,1,30,1024]{3,0,2,1:T(8,128)} async-done(((f32[16,8,30,1024]{3,0,2,1:T(8,128)}), f32[16,1,30,1024]{3,0,2,1:T(8,128)}) %reduce-scatter.2.cloned.1.call-update) | async-done | bytes 1966096 | tf_op jit(solution)/shard_map/reduce_scatter | solution.py:46
  302.8 4.9 %copy.84 = f32[16,1,30,1024]{3,1,2,0:T(1,128)} copy(f32[16,1,30,1024]{3,0,2,1:T(8,128)} %reduce-scatter.2.cloned.1.call-done) | data formatting | bytes 3932160 | tf_op jit(solution)/shard_map/reduce_scatter | solution.py:46
  308.3 5.9 %fusion.33 = bf16[4,64,8,128]{3,1,2,0:T(8,128)(2,1)S(1)} fusion(bf16[4,256,8,128]{3,2,1,0:T(8,128)(2,1)S(1)} %bitcast.104, f32[4,8,64]{2,1,0:T(8,128)S(1)} %get-tuple-element.8, f32[4,8,64,256]{3,2,1,0:T(8,128)} %copy-done), kind=kOutput, calls=%fused_computation.39 | convolution fusion | flops 136055040 | bytes 4726784 | tf_op jit(solution)/shard_map/chmn,cnhd->cmhd/dot_general | solution.py:104
  315.4 82.1 %all-reduce.3.cloned.1.call-done = f32[16,1,30,1024]{3,1,2,0:T(1,128)} async-done(((f32[16,1,30,1024]{3,1,2,0:T(1,128)}), f32[16,1,30,1024]{3,1,2,0:T(1,128)}) %all-reduce.3.cloned.1.call-update) | async-done | bytes 1966096
  (93 shorter events, 40.3 us)
Async XLA Ops:
  7.2 134.3 %all-gather.3.cloned.1.call-start = ((), (), s32[]{:S(2)}) async-start(), calls=%async_computation.5 | async-start | bytes 4128768 | tf_op jit(solution)/shard_map/all_gather | solution.py:36
  9.1 143.3 %all-gather.5.cloned.1.call-start = ((), (), s32[]{:S(2)}) async-start(), calls=%async_computation.6 | async-start | bytes 4718592 | tf_op jit(solution)/shard_map/all_gather | solution.py:90
  43.9 56.6 %all-to-all-start.2 = ((bf16[16,8,16,896]{3,2,1,0:T(8,128)(2,1)}), bf16[16,8,16,896]{3,2,1,0:T(8,128)(2,1)}, u32[]{:S(2)}, u32[]{:S(2)}) async-start(bf16[16,8,16,896]{3,2,1,0:T(8,128)(2,1)} %bitcast.94), calls=%async_computation.2 | async-start | bytes 7340032 | tf_op jit(solution)/shard_map/all_to_all | solution.py:72
  104.6 4.7 %copy-start.13 = (bf16[256,2048]{1,0:T(8,128)(2,1)S(1)}, bf16[256,2048]{1,0:T(8,128)(2,1)}, u32[]{:S(2)}) copy-start(bf16[256,2048]{1,0:T(8,128)(2,1)} %param.7) | copy-start | bytes 3145732
  104.6 5.2 %copy-start.14 = (bf16[256,1024]{1,0:T(8,128)(2,1)S(1)}, bf16[256,1024]{1,0:T(8,128)(2,1)}, u32[]{:S(2)}) copy-start(bf16[256,1024]{1,0:T(8,128)(2,1)} %param.8) | copy-start | bytes 1572868
  104.6 28.8 %all-to-all-start.3 = ((bf16[8,8,16,896]{3,2,1,0:T(8,128)(2,1)}), bf16[8,8,16,896]{3,2,1,0:T(8,128)(2,1)}, u32[]{:S(2)}, u32[]{:S(2)}) async-start(bf16[8,8,16,896]{3,2,1,0:T(8,128)(2,1)} %bitcast.6), calls=%async_computation.3 | async-start | bytes 3670016 | tf_op jit(solution)/shard_map/all_to_all | solution.py:75
  109.1 193.8 %reduce-scatter.2.cloned.1.call-start = ((), (), s32[]{:S(2)}) async-start(), calls=%async_computation.7 | async-start | bytes 17694720 | tf_op jit(solution)/shard_map/reduce_scatter | solution.py:46
  145.3 2.8 copy-start.16
  152.4 3.7 copy-start.1
  156.1 0.9 copy-start.4
  157.0 2.0 copy-start
  165.7 3.5 copy-start.3
  169.2 1.0 copy-start.5
  170.2 1.6 copy-start.2
  171.8 1.8 copy-start.9
  183.0 4.3 %copy-start.10 = (bf16[1024,1024,1,1]{1,0,2,3:T(8,128)(2,1)S(1)}, bf16[1024,1024,1,1]{1,0,2,3:T(8,128)(2,1)}, u32[]{:S(2)}) copy-start(bf16[1024,1024,1,1]{1,0,2,3:T(8,128)(2,1)} %reshape.265) | copy-start | bytes 6291460
  187.4 6.9 %copy-start.11 = (bf16[1024,1024,1,1]{1,0,2,3:T(8,128)(2,1)S(1)}, bf16[1024,1024,1,1]{1,0,2,3:T(8,128)(2,1)}, u32[]{:S(2)}) copy-start(bf16[1024,1024,1,1]{1,0,2,3:T(8,128)(2,1)} %reshape.264) | copy-start | bytes 6291460
  187.4 6.9 %copy-start.12 = (bf16[16,8,7,1024]{3,2,1,0:T(8,128)(2,1)S(1)}, bf16[16,8,7,1024]{3,2,1,0:T(8,128)(2,1)}, u32[]{:S(2)}) copy-start(bf16[16,8,7,1024]{3,2,1,0:T(8,128)(2,1)} %dot_general.58) | copy-start | bytes 5505028
  194.3 5.3 %copy-start.15 = (bf16[4,64,8,128]{3,1,2,0:T(8,128)(2,1)S(1)}, bf16[4,64,8,128]{3,1,2,0:T(8,128)(2,1)}, u32[]{:S(2)}) copy-start(bf16[4,64,8,128]{3,1,2,0:T(8,128)(2,1)} %fusion.30) | copy-start | bytes 1572868
  200.2 2.2 copy-start.6
  200.2 3.5 copy-start.7
  219.0 88.7 %copy-start.17 = (u32[128]{0:T(128)S(1)}, u32[128]{0:T(128)}, u32[]{:S(2)}) copy-start(u32[128]{0:T(128)} %constant.54) | copy-start | bytes 1540
  219.1 89.3 %copy-start.8 = (bf16[128,8,8,128]{3,2,1,0:T(8,128)(2,1)S(1)}, bf16[128,8,8,128]{3,2,1,0:T(8,128)(2,1)}, u32[]{:S(2)}) copy-start(bf16[128,8,8,128]{3,2,1,0:T(8,128)(2,1)} %copy.97) | copy-start | bytes 6291460
  219.1 178.5 %all-reduce.3.cloned.1.call-start = ((), (), s32[]{:S(2)}) async-start(), calls=%async_computation.8 | async-start | bytes 3932160
Sparse Core Ops, SparseCore 0:
  9.7 32.3 all-gather.2
  43.8 31.9 all-gather.4
  219.2 83.6 reduce-scatter.1
  307.8 89.6 all-reduce.2
where the time goes:
time: 409 us; the launch traced here: 408 us
  waiting for transfers between devices  241 us (59%)
  local copies, waits for them, and re-layouts  66 us (16%)
  matrix products  42.2 us (10%)
  blocking collectives  24.9 us (6%)
  between operations  14.1 us (3%)
  other arithmetic  11 us (3%)
  starting transfers between devices  9.3 us (2%)
    reduce_scatter x1, waiting for transfers between devices, side_by_side(): whole = lax.psum_scatter(both, axis, scatter_dimension=dim, tiled=True)  83.7 us
    unnamed x5, waiting for transfers between devices  82.9 us
    all_to_all x1, waiting for transfers between devices, body(): lax.all_to_all(fetched, 'dp', split_axis=0, concat_axis=0, tiled=True)  52 us
    all_to_all x1, waiting for transfers between devices, body(): lax.all_to_all(chosen, 'shard', split_axis=0, concat_axis=2, tiled=True)  22.2 us
    all_to_all x1, blocking collectives, body(): lax.all_to_all(outgoing, 'dp', split_axis=0, concat_axis=0, tiled=True)  15.3 us
    unnamed x46, local copies, waits for them, and re-layouts  13.5 us
    concatenate x1, local copies, waits for them, and re-layouts, side_by_side(): both = jnp.concatenate(arrays, axis=along)  11.4 us
    all_to_all x1, blocking collectives, copy_for_each(): lax.all_to_all(jnp.broadcast_to(array[None], (count, *array.shape)), axis...  9.66 us
  transfers between devices with their start and end apart: 6, of which 4 were waited for; matrix products, arithmetic and copies ran while one was open for 10% of the time, Pallas kernels for 0%

commit v1 on v0

v1 whole, which is shorter than its diff:
```python
import functools

import jax
import jax.numpy as jnp
from jax import lax
from jax.experimental import pallas as pl
from jax.experimental.pallas import tpu as pltpu
from jax.sharding import PartitionSpec as P

LAT = 896
HEADS = 8
HEAD_DIM = 128
SPAN = 64
NBR = 2
NT = 128
CH_DEV = 4
INNER = 1024
D = 2048
CHIPS = 64
PARTS = ((0, 384), (384, 384), (768, 256))
WIDTHS = tuple(w for _, w in PARTS) * 2
LEVELS = 6
OFFSETS = (0, 32, 48, 56, 60, 62)
NT_DIMS = (((1,), (1,)), ((), ()))
MESH = pl.DeviceIdType.MESH


def nt_dot(a, b):
    return lax.dot_general(a, b, NT_DIMS, preferred_element_type=jnp.float32)


def nn_dot(a, b):
    return jnp.dot(a, b, preferred_element_type=jnp.float32)


def place(chip, part):
    code = chip ^ ((chip >> 1) & 21)
    return ((code << part) | (code >> (LEVELS - part))) & (CHIPS - 1)


def one_hot(rows, columns, wanted):
    r = lax.broadcasted_iota(jnp.int32, (rows, columns), 0)
    c = lax.broadcasted_iota(jnp.int32, (rows, columns), 1)
    return wanted(r, c).astype(jnp.float32).astype(jnp.bfloat16)


def compute_kernel(
    tok, cot, lat, wq, wk, wv, ctx, x0, x1, x2, x3, x4, x5, normed, q, kb, vb, qg, kg, vg, lat_t
):
    scale = HEAD_DIM ** (-0.5)
    outs = (x0, x1, x2, x3, x4, x5)

    @pl.loop(0, 8)
    def _(i):
        rows = pl.ds(pl.multiple_of(i * 32, 32), 32)
        t = tok[rows, :].astype(jnp.float32)
        inverse = lax.rsqrt(jnp.mean(t * t, axis=-1, keepdims=True) + 1e-06)
        normed[rows, :] = (t * inverse).astype(jnp.bfloat16)

    @pl.loop(0, 4)
    def _(i):
        cols = pl.ds(pl.multiple_of(i * 256, 256), 256)
        q[:, cols] = (nn_dot(normed[...], wq[:, cols]) * scale).astype(jnp.bfloat16)

    eye = one_hot(128, 128, lambda r, c: r == c)
    zero = jnp.zeros((SPAN, HEAD_DIM), jnp.bfloat16)

    def diagonal(ref, rows, at):
        a = ref[rows, at : at + HEAD_DIM]
        b = ref[rows, at + HEAD_DIM : at + 2 * HEAD_DIM]
        return jnp.concatenate(
            [jnp.concatenate([a, zero], axis=1), jnp.concatenate([zero, b], axis=1)], axis=0
        )

    @pl.loop(0, CH_DEV)
    def _(c):
        rows = pl.ds(pl.multiple_of(c * 256, 256), 256)
        trows = pl.ds(pl.multiple_of(c * SPAN, SPAN), SPAN)
        block = lat[rows, :]
        for at in range(0, INNER, 256):
            kb[:, at : at + 256] = nn_dot(block, wk[:, at : at + 256]).astype(jnp.bfloat16)
            vb[:, at : at + 256] = nn_dot(block, wv[:, at : at + 256]).astype(jnp.bfloat16)
        for at in range(0, INNER, 256):
            mid = at + HEAD_DIM
            end = at + 256
            kp = kb[:, at:end]
            vp = vb[:, at:end]
            q2 = diagonal(q, trows, at)
            g2 = diagonal(cot, trows, at)
            scores = nt_dot(kp, q2)
            e = jnp.exp(scores - jnp.max(scores, axis=0, keepdims=True))
            prob = e * (1.0 / jnp.sum(e, axis=0, keepdims=True))
            prob_t = prob.astype(jnp.bfloat16)
            prob_r = nt_dot(eye, prob_t).astype(jnp.bfloat16)
            c2 = nn_dot(prob_r, vp).astype(jnp.bfloat16)
            ctx[trows, at:mid] = c2[:SPAN, :HEAD_DIM]
            ctx[trows, mid:end] = c2[SPAN:, HEAD_DIM:]
            vg[rows, at:end] = nn_dot(prob_t, g2).astype(jnp.bfloat16)
            pg = nt_dot(vp, g2)
            sg_t = (prob * (pg - jnp.sum(prob * pg, axis=0, keepdims=True))).astype(jnp.bfloat16)
            kg[rows, at:end] = nn_dot(sg_t, q2).astype(jnp.bfloat16)
            sg = nt_dot(eye, sg_t).astype(jnp.bfloat16)
            qg2 = (nn_dot(sg, kp) * scale).astype(jnp.bfloat16)
            qg[trows, at:mid] = qg2[:SPAN, :HEAD_DIM]
            qg[trows, mid:end] = qg2[SPAN:, HEAD_DIM:]

    eye_wide = one_hot(256, 256, lambda r, c: r == c)

    @pl.loop(0, 8)
    def _(i):
        cols = pl.ds(pl.multiple_of(i * 256, 256), 256)
        turned = nt_dot(eye_wide, normed[:, cols]).astype(jnp.bfloat16)
        for p, (at, width) in enumerate(PARTS):
            r = nn_dot(turned, qg[:, at : at + width]).astype(jnp.bfloat16)
            for j in range(16):
                outs[p][j & 1, place(8 * i + (j >> 1), p)] = r[16 * j : 16 * j + 16, :]

    for b, (at, width) in enumerate(((0, 256), (128, 384), (384, 384), (640, 256))):
        pick = one_hot(
            256,
            width,
            lambda r, c: (c + at == 224 * b + 7 * (r >> 3) + (r & 7)) & ((r & 7) < 7),
        )
        for rat in range(0, 1024, 256):
            lat_t[256 * b : 256 * b + 256, rat : rat + 256] = nt_dot(
                pick, lat[rat : rat + 256, at : at + width]
            ).astype(jnp.bfloat16)

    @pl.loop(0, 4)
    def _(b):
        rows = pl.ds(pl.multiple_of(b * 256, 256), 256)
        turned = lat_t[rows, :]
        for p, (at, width) in enumerate(PARTS):
            rk = nn_dot(turned, kg[:, at : at + width])
            rv = nn_dot(turned, vg[:, at : at + width])
            for j in range(32):
                both = jnp.concatenate([rk[8 * j : 8 * j + 8], rv[8 * j : 8 * j + 8]], axis=0)
                outs[3 + p][j & 1, place(16 * b + (j >> 1), 3 + p)] = both.astype(jnp.bfloat16)


def compute(tok, cot, lat, wq, wk, wv):
    bf = jnp.bfloat16
    vmem = pl.BlockSpec(memory_space=pltpu.VMEM)
    return pl.pallas_call(
        compute_kernel,
        out_shape=(
            jax.ShapeDtypeStruct((256, INNER), bf),
            *(jax.ShapeDtypeStruct((2, CHIPS, 16, w), bf) for w in WIDTHS),
        ),
        in_specs=[vmem] * 6,
        out_specs=(vmem,) * 7,
        scratch_shapes=[
            pltpu.VMEM((256, D), bf),
            pltpu.VMEM((256, INNER), bf),
            pltpu.VMEM((256, INNER), bf),
            pltpu.VMEM((256, INNER), bf),
            pltpu.VMEM((256, INNER), bf),
            pltpu.VMEM((1024, INNER), bf),
            pltpu.VMEM((1024, INNER), bf),
            pltpu.VMEM((1024, 1024), bf),
        ],
        compiler_params=pltpu.CompilerParams(vmem_limit_bytes=48 * 1024 * 1024),
        name="attend",
    )(tok, cot, lat, wq, wk, wv)


def flip(coordinate, high):
    return 3 - coordinate if high else coordinate ^ 1


def reduce_kernel(*refs):
    xs, (gq, gk, gv) = refs[:6], refs[6:9]
    crecv, acc, snd, rcv = refs[9:15], refs[15:21], refs[21:27], refs[27:33]
    csem, send_sem, recv_sem = refs[33:]
    dp = lax.axis_index("dp")
    shard = lax.axis_index("shard")
    z, x, y, core = dp // 4, dp % 4, shard // 2, shard % 2
    other = (dp, y * 2 + (1 - core))
    partners = []
    for d in range(LEVELS):
        high = d % 2 == 0
        if d < 2:
            partners.append((flip(z, high) * 4 + x, shard))
        elif d < 4:
            partners.append((z * 4 + flip(x, high), shard))
        else:
            partners.append((dp, flip(y, high) * 2 + core))
    mine = place(z * 16 + x * 4 + y, 0)

    barrier = pltpu.get_barrier_semaphore()
    for device in [other] + partners:
        pl.semaphore_signal(barrier, inc=1, device_id=device, device_id_type=MESH)
    pl.semaphore_wait(barrier, 7)

    pending = []
    first = []
    for p in range(6):
        copy = pltpu.make_async_remote_copy(
            src_ref=xs[p].at[1 - core],
            dst_ref=crecv[p],
            send_sem=csem.at[0, p],
            recv_sem=csem.at[1, p],
            device_id=other,
            device_id_type=MESH,
        )
        copy.start()
        first.append(copy)
        pending.append(copy)
    coming = first
    base = [0] * 6
    for k in range(LEVELS):
        half = CHIPS >> (k + 1)
        step = min(half, 8)
        started = []
        for p in range(6):
            d = (p + k) % LEVELS
            bit = (mine >> (LEVELS - 1 - d)) & 1
            away = base[p] + (1 - bit) * half
            keep = base[p] + bit * half
            coming[p].wait_recv()

            def summed(at, p=p, k=k, step=step):
                where = pl.ds(at, step)
                if k == 0:
                    return xs[p][core, where].astype(jnp.float32) + crecv[p][where].astype(
                        jnp.float32
                    )
                back = pl.ds(OFFSETS[k - 1] + at - base[p], step)
                return acc[p][where] + rcv[p][back].astype(jnp.float32)

            @pl.loop(0, half // step)
            def _(i, p=p, k=k, away=away, step=step, summed=summed):
                snd[p][pl.ds(OFFSETS[k] + i * step, step)] = summed(away + i * step).astype(
                    jnp.bfloat16
                )

            copy = pltpu.make_async_remote_copy(
                src_ref=snd[p].at[pl.ds(OFFSETS[k], half)],
                dst_ref=rcv[p].at[pl.ds(OFFSETS[k], half)],
                send_sem=send_sem.at[k, p],
                recv_sem=recv_sem.at[k, p],
                device_id=partners[d],
                device_id_type=MESH,
            )
            copy.start()
            started.append(copy)
            pending.append(copy)

            @pl.loop(0, half // step)
            def _(i, p=p, keep=keep, step=step, summed=summed):
                acc[p][pl.ds(keep + i * step, step)] = summed(keep + i * step)

            base[p] = keep
        coming = started
    for p in range(6):
        coming[p].wait_recv()
        total = acc[p][base[p]] + rcv[p][OFFSETS[5]].astype(jnp.float32)
        at, width = PARTS[p % 3]
        if p < 3:
            gq[:, at : at + width] = total
        else:
            gk[:, at : at + width] = total[0:7]
            gv[:, at : at + width] = total[8:15]
    for copy in pending:
        copy.wait_send()


def reduce_scatter(xs):
    vmem = pl.BlockSpec(memory_space=pltpu.VMEM)
    f32, bf = jnp.float32, jnp.bfloat16
    return pl.pallas_call(
        reduce_kernel,
        out_shape=(
            jax.ShapeDtypeStruct((16, INNER), f32),
            jax.ShapeDtypeStruct((7, INNER), f32),
            jax.ShapeDtypeStruct((7, INNER), f32),
        ),
        in_specs=[vmem] * 6,
        out_specs=(vmem,) * 3,
        scratch_shapes=[
            *(pltpu.VMEM((CHIPS, 16, w), bf) for w in WIDTHS),
            *(pltpu.VMEM((CHIPS, 16, w), f32) for w in WIDTHS),
            *(pltpu.VMEM((CHIPS, 16, w), bf) for w in WIDTHS),
            *(pltpu.VMEM((CHIPS, 16, w), bf) for w in WIDTHS),
            pltpu.SemaphoreType.DMA((2, 6)),
            pltpu.SemaphoreType.DMA((LEVELS, 6)),
            pltpu.SemaphoreType.DMA((LEVELS, 6)),
        ],
        compiler_params=pltpu.CompilerParams(
            collective_id=1, has_side_effects=True, vmem_limit_bytes=40 * 1024 * 1024
        ),
        name="reduce_halving",
    )(*xs)


def copy_for_each(array, axis):
    count = lax.axis_size(axis)
    return lax.all_to_all(
        jnp.broadcast_to(array[None], (count, *array.shape)), axis, 0, 0, tiled=True
    )


def laid_out(parts, dim):
    parts = jnp.moveaxis(parts, 0, dim)
    dims = parts.shape
    return parts.reshape(*dims[:dim], dims[dim] * dims[dim + 1], *dims[dim + 2 :])


def collect(array, axis, dim):
    parts = copy_for_each(array, axis)
    return laid_out(parts, dim)


def sent_together(arrays, axis, dim, along):
    both = jnp.concatenate(arrays, axis=along)
    whole, at, gathered = (lax.all_gather(both, axis, axis=dim, tiled=True), 0, [])
    for a in arrays:
        gathered.append(lax.slice_in_dim(whole, at, at + a.shape[along], axis=along))
        at += a.shape[along]
    return tuple(gathered)


def body(tokens, ctx_cotangent, latent_cache, nbr_ids, w_query, w_key, w_value):
    owner_count = lax.axis_size("dp")
    shard_count = lax.axis_size("shard")
    owner_rows = latent_cache.shape[0]
    slice_tokens = latent_cache.shape[1]
    requests = nbr_ids.reshape(-1)
    gathered = collect(requests, "shard", 0)
    slot_count = 2 * gathered.shape[0] // owner_count
    owner_of = gathered // owner_rows
    within_row = gathered % owner_rows
    onehot = (owner_of[:, None] == jnp.arange(owner_count, dtype=jnp.int32)[None, :]).astype(
        jnp.int32
    )
    earlier = jnp.cumsum(onehot, axis=0) - onehot
    position = jnp.sum(earlier * onehot, axis=1)
    slot_of = owner_of * slot_count + position
    outgoing = jnp.zeros((owner_count * slot_count,), jnp.int32).at[slot_of].set(within_row)
    outgoing = outgoing.reshape(owner_count, slot_count)
    asked_rows = lax.all_to_all(outgoing, "dp", split_axis=0, concat_axis=0, tiled=True)
    fetched = latent_cache[asked_rows.reshape(-1)]
    fetched = fetched.reshape(asked_rows.shape[0], asked_rows.shape[1], slice_tokens, LAT)
    replies = lax.all_to_all(fetched, "dp", split_axis=0, concat_axis=0, tiled=True)
    arrived = replies.reshape(owner_count * slot_count, slice_tokens, LAT)
    chosen = arrived[slot_of].reshape(shard_count, -1, slice_tokens, LAT)
    latents = lax.all_to_all(chosen, "shard", split_axis=0, concat_axis=2, tiled=True)
    latent_rows = latents.reshape(-1, LAT)
    pieces = sent_together((w_key, w_value), "shard", 0, 1)
    whole_query = lax.all_gather(w_query, "shard", axis=0, tiled=True)
    context, *partial = compute(tokens, ctx_cotangent, latent_rows, whole_query, *pieces)
    return (context, *reduce_scatter(partial))


def solution(mesh):
    return jax.shard_map(
        body,
        mesh=mesh,
        in_specs=(
            P(("dp", "shard"), None),
            P(("dp", "shard"), None),
            P("dp", "shard", None),
            P(("dp", "shard"), None),
            P("shard", None),
            P("shard", None),
            P("shard", None),
        ),
        out_specs=(
            P(("dp", "shard"), None),
            P(("dp", "shard"), None),
            P(("dp", "shard"), None),
            P(("dp", "shard"), None),
        ),
        check_vma=False,
    )
```

time: 409 us -> 225 us (0.55)
  waiting for transfers between devices: 241 us -> 52.8 us
  Pallas kernels: 0 us -> 75.6 us
  local copies, waits for them, and re-layouts: 66 us -> 21.6 us
  matrix products: 42.2 us -> 0 us
  blocking collectives: 24.9 us -> 51.8 us
  other arithmetic: 11 us -> 3.57 us
  starting transfers between devices: 9.3 us -> 4.59 us
    reduce_scatter x1 -> x0, waiting for transfers between devices: 83.7 us -> none  [side_by_side(): whole = lax.psum_scatter(both, axis, scatter_dimension=dim, tiled=True)]
    unnamed x5 -> x2, waiting for transfers between devices: 82.9 us -> 0.71 us
    pallas_call x0 -> x2, Pallas kernels: none -> 75.6 us  [the longest x1 38.1 us: reduce_scatter(): pl.pallas_call(reduce_kernel, out_shape=(jax.ShapeDtypeStruct((16, INNER)...]
    dot_general x12 -> x0, matrix products: 42.2 us -> none  [the longest x1 6.93 us: body(): jnp.einsum('tl,te->le', latent_rows, value_grad, preferred_element_type=j...]
    all_to_all x0 -> x1, blocking collectives: none -> 26.8 us  [body(): lax.all_to_all(chosen, 'shard', split_axis=0, concat_axis=2, tiled=True)]
    all_to_all x1 -> x0, waiting for transfers between devices: 22.2 us -> none  [body(): lax.all_to_all(chosen, 'shard', split_axis=0, concat_axis=2, tiled=True)]
    concatenate x1 -> x0, local copies, waits for them, and re-layouts: 11.4 us -> none  [side_by_side(): both = jnp.concatenate(arrays, axis=along)]
    reshape x3 -> x0, local copies, waits for them, and re-layouts: 8.66 us -> none  [the longest x1 4.31 us: body(): key_grad = key_grad.reshape(-1, INNER)]
  transfers between devices with their start and end apart: 6 -> 3, of which waited for: 4 -> 1; matrix products, arithmetic and copies ran while one was open for 10% -> 8% of each run, Pallas kernels for 0% -> 0%
where the time goes in v1:
time: 225 us; the launch traced here: 224 us
  Pallas kernels  75.6 us (34%)
  waiting for transfers between devices  52.8 us (23%)
  blocking collectives  51.8 us (23%)
  local copies, waits for them, and re-layouts  21.6 us (10%)
  between operations  14.2 us (6%)
  starting transfers between devices  4.59 us (2%)
  other arithmetic  3.57 us (2%)
    all_to_all x1, waiting for transfers between devices, body(): lax.all_to_all(fetched, 'dp', split_axis=0, concat_axis=0, tiled=True)  52.1 us
    pallas_call x1, Pallas kernels, reduce_scatter(): pl.pallas_call(reduce_kernel, out_shape=(jax.ShapeDtypeStruct((16, INNER)...  38.1 us
    pallas_call x1, Pallas kernels, compute(): pl.pallas_call(compute_kernel, out_shape=(jax.ShapeDtypeStruct((256, INNE...  37.5 us
    all_to_all x1, blocking collectives, body(): lax.all_to_all(chosen, 'shard', split_axis=0, concat_axis=2, tiled=True)  26.8 us
    all_to_all x1, blocking collectives, body(): lax.all_to_all(outgoing, 'dp', split_axis=0, concat_axis=0, tiled=True)  15.3 us
    all_to_all x1, blocking collectives, copy_for_each(): lax.all_to_all(jnp.broadcast_to(array[None], (count, *array.shape)), axis...  9.66 us
    unnamed x16, local copies, waits for them, and re-layouts  6.19 us
    gather x1, local copies, waits for them, and re-layouts, body(): fetched = latent_cache[asked_rows.reshape(-1)]  4.9 us
  transfers between devices with their start and end apart: 3, of which 1 were waited for; matrix products, arithmetic and copies ran while one was open for 8% of the time, Pallas kernels for 0%

profile of v1, /device:TPU:0, one launch (start us, length us, event | category | flops | bytes accessed | tf_op | source)
XLA Modules:
  0.0 224.1 jit_solution(8471551586057436480)
XLA Ops:
  7.2 1.8 pad_maximum_fusion
  9.1 0.7 all-gather.3.cloned.1.call-update
  10.0 9.7 %all_to_all.35 = s32[8,1,8]{2,1,0:T(1,128)S(1)} all-to-all(s32[8,1,8]{2,1,0:T(1,128)S(1)} %broadcast_in_dim.5), channel_id=1, replica_groups=mesh['dp'=16,'shard'=8] {'shard'}, dimensions={0} | all-to-all | bytes 512 | tf_op jit(solution)/shard_map/all_to_all | solution.py:298
  19.8 0.5 broadcast.161
  20.3 0.7 reduce.8
  21.2 0.2 select_reduce_fusion
  21.4 0.8 scatter_custom_fusion
  22.3 15.3 %all_to_all.36 = s32[16,1,8]{2,1,0:T(1,128)S(1)} all-to-all(s32[16,1,8]{2,1,0:T(1,128)S(1)} %bitcast.23), channel_id=1, replica_groups=mesh['dp'=16,'shard'=8] {'dp'}, dimensions={0} | all-to-all | bytes 1024 | tf_op jit(solution)/shard_map/all_to_all | solution.py:341
  37.6 0.7 reduce.9
  38.4 4.9 %gather_fusion = bf16[128,16,896]{2,1,0:T(8,128)(2,1)} fusion(bf16[128,16,896]{2,1,0:T(8,128)(2,1)} %param.9, s32[1024]{0:T(1024)S(1)} %pad_clamp_fusion.1), kind=kCustom, calls=%fused_computation | custom fusion | bytes 7340544 | tf_op jit(solution)/shard_map/gather | solution.py:342
  43.3 4.5 %all-to-all-start.2 = ((bf16[16,8,16,896]{3,2,1,0:T(8,128)(2,1)}), bf16[16,8,16,896]{3,2,1,0:T(8,128)(2,1)}, u32[]{:S(2)}, u32[]{:S(2)}) async-start(bf16[16,8,16,896]{3,2,1,0:T(8,128)(2,1)} %bitcast.18), calls=%async_computation.2 | async-start | bytes 7340032 | tf_op jit(solution)/shard_map/all_to_all | solution.py:344
  47.8 52.1 %all-to-all-done.2 = bf16[16,8,16,896]{3,2,1,0:T(8,128)(2,1)} async-done(((bf16[16,8,16,896]{3,2,1,0:T(8,128)(2,1)}), bf16[16,8,16,896]{3,2,1,0:T(8,128)(2,1)}, u32[]{:S(2)}, u32[]{:S(2)}) %all-to-all-start.2) | async-done | bytes 3670048 | tf_op jit(solution)/shard_map/all_to_all | solution.py:344
  99.9 2.9 %gather_fusion.1 = bf16[64,16,896]{2,1,0:T(8,128)(2,1)S(1)} fusion(bf16[128,16,896]{2,1,0:T(8,128)(2,1)} %bitcast.5, s32[1024]{0:T(1024)S(1)} %pad_clamp_fusion), kind=kCustom, calls=%fused_computation.1 | custom fusion | bytes 3670272 | tf_op jit(solution)/shard_map/gather | solution.py:346
  102.8 26.8 %all_to_all.37 = bf16[8,8,16,896]{3,2,1,0:T(8,128)(2,1)S(1)} all-to-all(bf16[8,8,16,896]{3,2,1,0:T(8,128)(2,1)S(1)} %bitcast.20), channel_id=1, replica_groups=mesh['dp'=16,'shard'=8] {'shard'}, dimensions={0} | all-to-all | bytes 3670016 | tf_op jit(solution)/shard_map/all_to_all | solution.py:347
  129.6 1.5 copy.16
  131.1 4.4 %fusion.5 = (bf16[896,1024]{1,0:T(8,128)(2,1)}, bf16[896,1024]{1,0:T(8,128)(2,1)}) fusion(bf16[896,2048]{1,0:T(8,128)(2,1)} %all-gather.5.cloned.1.call-done), kind=kLoop, calls=%fused_computation.25 | loop fusion | bytes 7340032 | tf_op jit(solution)/shard_map/slice | solution.py:318
  135.5 37.5 %attend.1 = (bf16[256,1024]{1,0:T(8,128)(2,1)}, bf16[2,64,16,384]{3,2,1,0:T(8,128)(2,1)S(1)}, bf16[2,64,16,384]{3,2,1,0:T(8,128)(2,1)}, bf16[2,64,16,256]{3,2,1,...) custom-call(bf16[256,2048]{1,0:T(8,128)(2,1)S(1)} %copy-done.3, ...), custom_call_target="tpu_custom_call" | custom-call | tf_op jit(solution)/shard_map/attend/pallas_call | solution.py:144
  173.0 1.4 copy-done
  174.4 1.4 copy-done.1
  175.8 1.4 copy-done.2
  177.3 38.1 %reduce_halving.1 = (f32[16,1024]{1,0:T(8,128)S(1)}, f32[7,1024]{1,0:T(8,128)S(1)}, f32[7,1024]{1,0:T(8,128)S(1)}) custom-call(bf16[2,64,16,384]{3,2,1,0:T(8,128)(2,1)S(1)} %get-tuple-element.15.refs_0_, bf16[2,64,16,384]{3,2,1,0:T(8,128)(2,1)S(1)} %copy-done, bf16[2,64,16,256]{3,2,1,0:T(8,128)(2,1)S(1)} %get-tuple-element.17.refs_2_, ...), custom_call_target="tpu_custom_call" | custom-call | tf_op jit(solution)/shard_map/reduce_halving/pallas_call | solution.py:271
  215.4 0.6 copy.20
  216.0 0.6 copy.21
  216.7 0.6 copy.22
  (28 shorter events, 0.8 us)
Async XLA Ops:
  7.2 2.7 %copy-start.5 = (s32[4,2]{0,1:T(2,128)S(1)}, s32[4,2]{0,1:T(2,128)}, u32[]{:S(2)}) copy-start(s32[4,2]{0,1:T(2,128)} %param.10) | copy-start | bytes 100
  7.2 123.9 %all-gather.5.cloned.1.call-start = ((), (), s32[]{:S(2)}) async-start(), calls=%async_computation.5 | async-start | bytes 4128768 | tf_op jit(solution)/shard_map/all_gather | solution.py:316
  9.1 126.4 %all-gather.3.cloned.1.call-start = ((), (), s32[]{:S(2)}) async-start(), calls=%async_computation.4 | async-start | bytes 4718592 | tf_op jit(solution)/shard_map/all_gather | solution.py:350
  43.3 56.6 %all-to-all-start.2 = ((bf16[16,8,16,896]{3,2,1,0:T(8,128)(2,1)}), bf16[16,8,16,896]{3,2,1,0:T(8,128)(2,1)}, u32[]{:S(2)}, u32[]{:S(2)}) async-start(bf16[16,8,16,896]{3,2,1,0:T(8,128)(2,1)} %bitcast.18), calls=%async_computation.2 | async-start | bytes 7340032 | tf_op jit(solution)/shard_map/all_to_all | solution.py:344
  131.1 4.4 %copy-start.3 = (bf16[256,2048]{1,0:T(8,128)(2,1)S(1)}, bf16[256,2048]{1,0:T(8,128)(2,1)}, u32[]{:S(2)}) copy-start(bf16[256,2048]{1,0:T(8,128)(2,1)} %tok.1) | copy-start | bytes 3145732
  131.1 4.5 %copy-start.4 = (bf16[256,1024]{1,0:T(8,128)(2,1)S(1)}, bf16[256,1024]{1,0:T(8,128)(2,1)}, u32[]{:S(2)}) copy-start(bf16[256,1024]{1,0:T(8,128)(2,1)} %cot.1) | copy-start | bytes 1572868
  173.0 1.4 copy-start
  174.4 1.4 copy-start.1
  175.8 1.4 copy-start.2
Sparse Core Ops, SparseCore 0:
  10.2 32.3 all-gather.4
  44.4 31.9 all-gather.2

commit v2 on v1

v2 whole, which is shorter than its diff:
```python
import functools

import jax
import jax.numpy as jnp
from jax import lax
from jax.experimental import pallas as pl
from jax.experimental.pallas import tpu as pltpu
from jax.sharding import PartitionSpec as P

LAT = 896
HEADS = 8
HEAD_DIM = 128
SPAN = 64
NBR = 2
NT = 128
CH_DEV = 4
INNER = 1024
D = 2048
CHIPS = 64
PARTS = ((0, 384), (384, 384), (768, 256))
WIDTHS = tuple(w for _, w in PARTS) * 2
LEVELS = 6
CHUNKS = ((0, 384), (384, 256), (640, 256))
DP_ORDER = (1, 4, 3, 12, 2, 8, 5, 15, 7, 13, 6, 9, 11, 14, 10)
WEIGHT_ROWS = (256, 112, 112)
WEIGHT_CUTS = (128, 64, 48)
OFFSETS = (0, 32, 48, 56, 60, 62)
NT_DIMS = (((1,), (1,)), ((), ()))
MESH = pl.DeviceIdType.MESH


def nt_dot(a, b):
    return lax.dot_general(a, b, NT_DIMS, preferred_element_type=jnp.float32)


def nn_dot(a, b):
    return jnp.dot(a, b, preferred_element_type=jnp.float32)


def place(chip, part):
    code = chip ^ ((chip >> 1) & 21)
    return ((code << part) | (code >> (LEVELS - part))) & (CHIPS - 1)


def one_hot(rows, columns, wanted):
    r = lax.broadcasted_iota(jnp.int32, (rows, columns), 0)
    c = lax.broadcasted_iota(jnp.int32, (rows, columns), 1)
    return wanted(r, c).astype(jnp.float32).astype(jnp.bfloat16)


def running_count(mask, lane):
    for s in (1, 2, 4, 8, 16, 32):
        mask = mask + jnp.where(lane >= s, pltpu.roll(mask, s, 1), 0)
    return mask


def packed_left(mask, values, lane):
    shift = jnp.where(mask > 0, lane - running_count(mask, lane) + 1, 0)
    values = jnp.where(mask > 0, values, 0)
    for b in (1, 2, 4, 8, 16, 32):
        moves = (shift & b) > 0
        values = jnp.where(moves, 0, values) + pltpu.roll(jnp.where(moves, values, 0), 128 - b, 1)
        shift = jnp.where(moves, 0, shift) + pltpu.roll(jnp.where(moves, shift, 0), 128 - b, 1)
    return values


def flip(coordinate, high):
    return 3 - coordinate if high else coordinate ^ 1


def whole_kernel(
    id_row, tok_in, cot_in, cache_in, wq_in, wk_in, wv_in, ctx, gq, gk, gv, *scratch
):
    it = iter(scratch)

    def take(n=None):
        return next(it) if n is None else tuple(next(it) for _ in range(n))

    ids_shard, id_group, ids_dp, asked_v, slots_v, asked_s, slots_s = take(7)
    cache, tok, cot = take(3)
    weights = take(3)
    wq, wk, wv = weights
    outgoing, replies, chosen = take(3), take(3), take(3)
    lat = take()
    normed, q, kb, vb, qg, kg, vg, lat_t = take(8)
    xs, crecv, acc, snd, rcv = take(6), take(6), take(6), take(6), take(6)
    local_sem, id_send, id_recv, gid_send, gid_recv, w_send, w_recv = take(7)
    dp_send, dp_recv, sh_send, sh_recv, csem, send_sem, recv_sem = take(7)

    dp = lax.axis_index("dp")
    shard = lax.axis_index("shard")
    z, x, y, core = dp // 4, dp % 4, shard // 2, shard % 2
    other = (dp, y * 2 + (1 - core))
    pending = []

    def send(src, dst, ss, rs, device):
        copy = pltpu.make_async_remote_copy(
            src_ref=src,
            dst_ref=dst,
            send_sem=ss,
            recv_sem=rs,
            device_id=device,
            device_id_type=MESH,
        )
        copy.start()
        pending.append(copy)
        return copy

    barrier = pltpu.get_barrier_semaphore()
    for r in range(1, 8):
        pl.semaphore_signal(barrier, inc=1, device_id=(dp, shard ^ r), device_id_type=MESH)
    for r in DP_ORDER:
        pl.semaphore_signal(barrier, inc=1, device_id=(dp ^ r, shard), device_id_type=MESH)

    def w_rows(a, row, side, start=0, size=None):
        n = WEIGHT_ROWS[a]
        at = pl.multiple_of((row * 2 + side) * n + start, 16)
        return weights[a].at[pl.ds(at, n if size is None else size)]

    own_weights = []
    for a, src in enumerate((wq_in, wk_in, wv_in)):
        copy = pltpu.make_async_copy(src, w_rows(a, y, core), local_sem.at[a])
        copy.start()
        own_weights.append(copy)
    loads = []
    for n, (src, dst) in enumerate(((cache_in, cache), (tok_in, tok), (cot_in, cot))):
        copy = pltpu.make_async_copy(src, dst, local_sem.at[3 + n])
        copy.start()
        loads.append(copy)

    pl.semaphore_wait(barrier, 22)

    ids_shard[shard] = id_row[...]
    asks = [
        send(id_row, ids_shard.at[shard], id_send.at[r], id_recv.at[r], (dp, shard ^ r))
        for r in range(1, 8)
    ]
    for copy in asks:
        copy.wait_recv()
    group = ids_shard[0]
    for s in range(1, 8):
        group = group + ids_shard[s]
    id_group[...] = group
    ids_dp[dp] = group
    asks = [
        send(id_group, ids_dp.at[dp], gid_send.at[r], gid_recv.at[r], (dp ^ r, shard))
        for r in DP_ORDER
    ]

    up, down, far = (y + 1) % 4, (y + 3) % 4, (y + 2) % 4
    for copy in own_weights:
        copy.wait()
    kinds = {}

    def send_weights(kind, row, device, part=None):
        copies = []
        for a in range(3):
            n, cut = WEIGHT_ROWS[a], WEIGHT_CUTS[a]
            start, size = ((0, n), (0, cut), (cut, n - cut))[0 if part is None else 1 + part]
            ref = w_rows(a, row, core, start, size)
            copies.append(send(ref, ref, w_send.at[kind, a], w_recv.at[kind, a], device))
        kinds[kind] = copies

    def arrived(kind):
        for copy in kinds[kind]:
            copy.wait_recv()

    send_weights(0, y, (dp, up * 2 + core))
    send_weights(1, y, (dp, down * 2 + core))
    send_weights(2, y, other)

    lane = lax.broadcasted_iota(jnp.int32, (16, 128), 1)
    owners = lax.broadcasted_iota(jnp.int32, (16, 128), 0)
    mine = jnp.where((lane < 64) & ((group[0:1] >> 7) == owners), 1, 0)
    places = jnp.where(mine > 0, owners * 8 + running_count(mine, lane) - 1, 0)
    slots = places[0:1]
    for o in range(1, 16):
        slots = slots + places[o : o + 1]
    slots_v[...] = jnp.broadcast_to(slots, (8, 128))

    for copy in asks:
        copy.wait_recv()
    ids = jnp.concatenate([ids_dp[g][0:1] for g in range(16)], axis=0)
    wanted = jnp.where((lane < 64) & ((ids >> 7) == dp), 1, 0)
    asked_v[...] = packed_left(wanted, ids & 127, lane)
    to_scalar = [
        pltpu.make_async_copy(asked_v, asked_s, local_sem.at[6]),
        pltpu.make_async_copy(slots_v, slots_s, local_sem.at[7]),
    ]
    for copy in to_scalar:
        copy.start()
    loads[0].wait()
    for copy in to_scalar:
        copy.wait()

    @pl.loop(0, 16)
    def _(g):
        for j in range(8):
            row = asked_s[g, j]
            for c, (at, width) in enumerate(CHUNKS):
                outgoing[c][g, j] = cache[row, :, at : at + width]

    fetches = []
    for c in range(3):
        own = pl.ds(pl.multiple_of(dp * 8, 8), 8)
        fetches.append(
            [
                send(
                    outgoing[c].at[dp ^ r],
                    replies[c].at[own],
                    dp_send.at[c, r],
                    dp_recv.at[c, r],
                    (dp ^ r, shard),
                )
                for r in DP_ORDER
            ]
        )
    for c in range(3):
        replies[c][pl.ds(pl.multiple_of(dp * 8, 8), 8)] = outgoing[c][dp]

    loads[1].wait()
    loads[2].wait()

    @pl.loop(0, 8)
    def _(i):
        rows = pl.ds(pl.multiple_of(i * 32, 32), 32)
        t = tok[rows, :].astype(jnp.float32)
        inverse = lax.rsqrt(jnp.mean(t * t, axis=-1, keepdims=True) + 1e-06)
        normed[rows, :] = (t * inverse).astype(jnp.bfloat16)

    spread = []

    def hand_on(c):
        at, width = CHUNKS[c]
        for copy in fetches[c]:
            copy.wait_recv()

        @pl.loop(0, 8)
        def _(s):
            for i in range(8):
                chosen[c][s, i] = replies[c][slots_s[0, s * 8 + i]]

        for r in range(1, 8):
            spread.append(
                send(
                    chosen[c].at[shard ^ r],
                    lat.at[:, shard, :, pl.ds(at, width)],
                    sh_send.at[c, r],
                    sh_recv.at[c, r],
                    (dp, shard ^ r),
                )
            )
        lat[:, shard, :, at : at + width] = chosen[c][shard]

    arrived(0)
    send_weights(3, down, (dp, up * 2 + core), 0)
    send_weights(5, down, other)
    arrived(1)
    send_weights(4, up, (dp, down * 2 + core), 1)
    send_weights(6, up, other)
    hand_on(0)
    arrived(3)
    send_weights(7, far, other, 0)
    arrived(4)
    send_weights(8, far, other, 1)
    hand_on(1)
    for kind in (2, 5, 6, 7, 8):
        arrived(kind)

    scale = HEAD_DIM ** (-0.5)

    @pl.loop(0, 4)
    def _(i):
        cols = pl.ds(pl.multiple_of(i * 256, 256), 256)
        q[:, cols] = (nn_dot(normed[...], wq[:, cols]) * scale).astype(jnp.bfloat16)

    hand_on(2)
    for copy in spread:
        copy.wait_recv()

    eye = one_hot(128, 128, lambda r, c: r == c)
    zero = jnp.zeros((SPAN, HEAD_DIM), jnp.bfloat16)

    def diagonal(ref, rows, at):
        a = ref[rows, at : at + HEAD_DIM]
        b = ref[rows, at + HEAD_DIM : at + 2 * HEAD_DIM]
        return jnp.concatenate(
            [jnp.concatenate([a, zero], axis=1), jnp.concatenate([zero, b], axis=1)], axis=0
        )

    @pl.loop(0, CH_DEV)
    def _(c):
        rows = pl.ds(pl.multiple_of(c * 256, 256), 256)
        trows = pl.ds(pl.multiple_of(c * SPAN, SPAN), SPAN)
        block = lat[pl.ds(2 * c, 2)].reshape(256, LAT)
        for at in range(0, INNER, 256):
            kb[:, at : at + 256] = nn_dot(block, wk[:, at : at + 256]).astype(jnp.bfloat16)
            vb[:, at : at + 256] = nn_dot(block, wv[:, at : at + 256]).astype(jnp.bfloat16)
        for at in range(0, INNER, 256):
            mid = at + HEAD_DIM
            end = at + 256
            kp = kb[:, at:end]
            vp = vb[:, at:end]
            q2 = diagonal(q, trows, at)
            g2 = diagonal(cot, trows, at)
            scores = nt_dot(kp, q2)
            e = jnp.exp(scores - jnp.max(scores, axis=0, keepdims=True))
            prob = e * (1.0 / jnp.sum(e, axis=0, keepdims=True))
            prob_t = prob.astype(jnp.bfloat16)
            prob_r = nt_dot(eye, prob_t).astype(jnp.bfloat16)
            c2 = nn_dot(prob_r, vp).astype(jnp.bfloat16)
            ctx[trows, at:mid] = c2[:SPAN, :HEAD_DIM]
            ctx[trows, mid:end] = c2[SPAN:, HEAD_DIM:]
            vg[rows, at:end] = nn_dot(prob_t, g2).astype(jnp.bfloat16)
            pg = nt_dot(vp, g2)
            sg_t = (prob * (pg - jnp.sum(prob * pg, axis=0, keepdims=True))).astype(jnp.bfloat16)
            kg[rows, at:end] = nn_dot(sg_t, q2).astype(jnp.bfloat16)
            sg = nt_dot(eye, sg_t).astype(jnp.bfloat16)
            qg2 = (nn_dot(sg, kp) * scale).astype(jnp.bfloat16)
            qg[trows, at:mid] = qg2[:SPAN, :HEAD_DIM]
            qg[trows, mid:end] = qg2[SPAN:, HEAD_DIM:]

    partners = []
    for d in range(LEVELS):
        high = d % 2 == 0
        if d < 2:
            partners.append((flip(z, high) * 4 + x, shard))
        elif d < 4:
            partners.append((z * 4 + flip(x, high), shard))
        else:
            partners.append((dp, flip(y, high) * 2 + core))
    here = place(z * 16 + x * 4 + y, 0)
    coming = [None] * 6
    base = [0] * 6
    root = [0] * 6

    def to_other_core(p):
        coming[p] = send(xs[p].at[1 - core], crecv[p], csem.at[0, p], csem.at[1, p], other)

    def halve(k, p):
        half = CHIPS >> (k + 1)
        step = min(half, 8)
        d = (p + k) % LEVELS
        bit = (here >> (LEVELS - 1 - d)) & 1
        away = base[p] + (1 - bit) * half
        keep = base[p] + bit * half
        coming[p].wait_recv()
        if k == 0:
            root[p] = keep

        def summed(at):
            where = pl.ds(at, step)
            if k == 0:
                return xs[p][core, where].astype(jnp.float32) + crecv[p][where].astype(jnp.float32)
            back = pl.ds(OFFSETS[k - 1] + at - base[p], step)
            return acc[p][pl.ds(at - root[p], step)] + rcv[p][back].astype(jnp.float32)

        @pl.loop(0, half // step)
        def _(i):
            snd[p][pl.ds(OFFSETS[k] + i * step, step)] = summed(away + i * step).astype(
                jnp.bfloat16
            )

        span = pl.ds(OFFSETS[k], half)
        copy = send(
            snd[p].at[span], rcv[p].at[span], send_sem.at[k, p], recv_sem.at[k, p], partners[d]
        )

        @pl.loop(0, half // step)
        def _(i):
            acc[p][pl.ds(keep - root[p] + i * step, step)] = summed(keep + i * step)

        base[p] = keep
        coming[p] = copy

    eye_wide = one_hot(256, 256, lambda r, c: r == c)

    @pl.loop(0, 8)
    def _(i):
        cols = pl.ds(pl.multiple_of(i * 256, 256), 256)
        turned = nt_dot(eye_wide, normed[:, cols]).astype(jnp.bfloat16)
        for p, (at, width) in enumerate(PARTS):
            r = nn_dot(turned, qg[:, at : at + width]).astype(jnp.bfloat16)
            for j in range(16):
                xs[p][j & 1, place(8 * i + (j >> 1), p)] = r[16 * j : 16 * j + 16, :]

    for p in range(3):
        to_other_core(p)

    for b, (at, width) in enumerate(((0, 256), (128, 384), (384, 384), (640, 256))):
        pick = one_hot(
            256,
            width,
            lambda r, c: (c + at == 224 * b + 7 * (r >> 3) + (r & 7)) & ((r & 7) < 7),
        )
        for n in range(4):
            block = lat[2 * n : 2 * n + 2, :, :, at : at + width].reshape(256, width)
            lat_t[256 * b : 256 * b + 256, 256 * n : 256 * n + 256] = nt_dot(pick, block).astype(
                jnp.bfloat16
            )

    for p in range(3):
        halve(0, p)

    for p, (at, width) in enumerate(PARTS):

        @pl.loop(0, 4)
        def _(b):
            turned = lat_t[pl.ds(pl.multiple_of(b * 256, 256), 256), :]
            rk = nn_dot(turned, kg[:, at : at + width])
            rv = nn_dot(turned, vg[:, at : at + width])
            for j in range(32):
                both = jnp.concatenate([rk[8 * j : 8 * j + 8], rv[8 * j : 8 * j + 8]], axis=0)
                xs[3 + p][j & 1, place(16 * b + (j >> 1), 3 + p)] = both.astype(jnp.bfloat16)

        to_other_core(3 + p)

    for p in range(3, 6):
        halve(0, p)
    for k in range(1, LEVELS):
        for p in range(6):
            halve(k, p)
    for p in range(6):
        coming[p].wait_recv()
        total = acc[p][base[p] - root[p]] + rcv[p][OFFSETS[5]].astype(jnp.float32)
        at, width = PARTS[p % 3]
        if p < 3:
            gq[:, at : at + width] = total
        else:
            gk[:, at : at + width] = total[0:7]
            gv[:, at : at + width] = total[8:15]
    for copy in pending:
        copy.wait_send()


def body(tokens, ctx_cotangent, latent_cache, nbr_ids, w_query, w_key, w_value):
    lane = jnp.arange(128, dtype=jnp.int32)
    id_row = jnp.where(
        lane // 8 == lax.axis_index("shard"), jnp.tile(nbr_ids.reshape(-1), 16), 0
    )
    id_row = jnp.broadcast_to(id_row[None], (8, 128))
    f32, bf, i32 = jnp.float32, jnp.bfloat16, jnp.int32
    vmem = pl.BlockSpec(memory_space=pltpu.VMEM)
    hbm = pl.BlockSpec(memory_space=pl.ANY)
    dma = pltpu.SemaphoreType.DMA
    widths = [w for _, w in CHUNKS]
    return pl.pallas_call(
        whole_kernel,
        out_shape=(
            jax.ShapeDtypeStruct((256, INNER), bf),
            jax.ShapeDtypeStruct((16, INNER), f32),
            jax.ShapeDtypeStruct((7, INNER), f32),
            jax.ShapeDtypeStruct((7, INNER), f32),
        ),
        in_specs=[vmem] + [hbm] * 6,
        out_specs=(vmem,) * 4,
        scratch_shapes=[
            pltpu.VMEM((8, 8, 128), i32),
            pltpu.VMEM((8, 128), i32),
            pltpu.VMEM((16, 8, 128), i32),
            pltpu.VMEM((16, 128), i32),
            pltpu.VMEM((8, 128), i32),
            pltpu.SMEM((16, 128), i32),
            pltpu.SMEM((8, 128), i32),
            pltpu.VMEM((128, 16, LAT), bf),
            pltpu.VMEM((256, D), bf),
            pltpu.VMEM((256, INNER), bf),
            pltpu.VMEM((D, INNER), bf),
            pltpu.VMEM((LAT, INNER), bf),
            pltpu.VMEM((LAT, INNER), bf),
            *(pltpu.VMEM((16, 8, 16, w), bf) for w in widths),
            *(pltpu.VMEM((128, 16, w), bf) for w in widths),
            *(pltpu.VMEM((8, 8, 16, w), bf) for w in widths),
            pltpu.VMEM((8, 8, 16, LAT), bf),
            pltpu.VMEM((256, D), bf),
            pltpu.VMEM((256, INNER), bf),
            pltpu.VMEM((256, INNER), bf),
            pltpu.VMEM((256, INNER), bf),
            pltpu.VMEM((256, INNER), bf),
            pltpu.VMEM((1024, INNER), bf),
            pltpu.VMEM((1024, INNER), bf),
            pltpu.VMEM((1024, 1024), bf),
            *(pltpu.VMEM((2, CHIPS, 16, w), bf) for w in WIDTHS),
            *(pltpu.VMEM((CHIPS, 16, w), bf) for w in WIDTHS),
            *(pltpu.VMEM((CHIPS // 2, 16, w), f32) for w in WIDTHS),
            *(pltpu.VMEM((CHIPS, 16, w), bf) for w in WIDTHS),
            *(pltpu.VMEM((CHIPS, 16, w), bf) for w in WIDTHS),
            dma((8,)),
            dma((8,)),
            dma((8,)),
            dma((16,)),
            dma((16,)),
            dma((9, 3)),
            dma((9, 3)),
            dma((3, 16)),
            dma((3, 16)),
            dma((3, 8)),
            dma((3, 8)),
            dma((2, 6)),
            dma((LEVELS, 6)),
            dma((LEVELS, 6)),
        ],
        compiler_params=pltpu.CompilerParams(
            collective_id=1, has_side_effects=True, vmem_limit_bytes=67043328
        ),
        name="retro",
    )(
        id_row,
        tokens,
        ctx_cotangent,
        latent_cache,
        w_query,
        w_key,
        w_value,
    )


def solution(mesh):
    return jax.shard_map(
        body,
        mesh=mesh,
        in_specs=(
            P(("dp", "shard"), None),
            P(("dp", "shard"), None),
            P("dp", "shard", None),
            P(("dp", "shard"), None),
            P("shard", None),
            P("shard", None),
            P("shard", None),
        ),
        out_specs=(
            P(("dp", "shard"), None),
            P(("dp", "shard"), None),
            P(("dp", "shard"), None),
            P(("dp", "shard"), None),
        ),
        check_vma=False,
    )
```

time: 225 us -> 148 us (0.66)
  Pallas kernels: 75.6 us -> 139 us
  waiting for transfers between devices: 52.8 us -> 0 us
  blocking collectives: 51.8 us -> 0 us
  local copies, waits for them, and re-layouts: 21.6 us -> 7.63 us
  between operations: 14.2 us -> 0.66 us
  starting transfers between devices: 4.59 us -> 0 us
  other arithmetic: 3.57 us -> 0.01 us
    pallas_call x2 -> x1, Pallas kernels: 75.6 us -> 139 us  [body(): pl.pallas_call(whole_kernel, out_shape=(jax.ShapeDtypeStruct((256, INNER)...]
    all_to_all x1 -> x0, waiting for transfers between devices: 52.1 us -> none  [body(): lax.all_to_all(fetched, 'dp', split_axis=0, concat_axis=0, tiled=True)]
    all_to_all x3 -> x0, blocking collectives: 51.8 us -> none  [the longest x1 26.8 us: body(): lax.all_to_all(chosen, 'shard', split_axis=0, concat_axis=2, tiled=True)]
    gather x2 -> x0, local copies, waits for them, and re-layouts: 7.78 us -> none  [the longest x1 4.9 us: body(): fetched = latent_cache[asked_rows.reshape(-1)]]
    all_to_all x1 -> x0, starting transfers between devices: 4.51 us -> none  [body(): lax.all_to_all(fetched, 'dp', split_axis=0, concat_axis=0, tiled=True)]
    slice x1 -> x0, local copies, waits for them, and re-layouts: 4.44 us -> none  [sent_together(): lax.slice_in_dim(whole, at, at + a.shape[along], axis=along)]
    unnamed x16 -> x5, local copies, waits for them, and re-layouts: 6.19 us -> 6.86 us
  transfers between devices with their start and end apart: 3 -> 0, of which waited for: 1 -> 0; matrix products, arithmetic and copies ran while one was open for 8% -> 0% of each run, Pallas kernels for 0% -> 0%
where the time goes in v2:
time: 148 us; the launch traced here: 147 us
  Pallas kernels  139 us (94%)
  local copies, waits for them, and re-layouts  7.63 us (5%)
    pallas_call x1, Pallas kernels, body(): pl.pallas_call(whole_kernel, out_shape=(jax.ShapeDtypeStruct((256, INNER)...  139 us
    unnamed x5, local copies, waits for them, and re-layouts  6.86 us

profile of v2, /device:TPU:0, one launch (start us, length us, event | category | flops | bytes accessed | tf_op | source)
XLA Modules:
  0.0 147.3 jit_solution(16811743810280584144)
XLA Ops:
  0.6 0.8 copy.12
  1.4 0.1 tile.10
  1.5 0.1 tile.12
  1.6 0.6 broadcast_in_dim.4.id_row
  2.2 139.0 %retro.1 = (bf16[256,1024]{1,0:T(8,128)(2,1)}, f32[16,1024]{1,0:T(8,128)}, f32[7,1024]{1,0:T(8,128)}, f32[7,1024]{1,0:T(8,128)}) custom-call(s32[8,128]{1,0:T(8,128)} %broadcast_in_dim.4.id_row, bf16[256,2048]{1,0:T(8,128)(2,1)} %tok_in.1, bf16[256,1024]{1,0:T(8,128)(2,1)} %cot_in.1, bf16[128,16,896]{2,1,0:T(8,128)(2,1)} %cache_in.1, ...), custom_call_target="tpu_custom_call" | custom-call | tf_op jit(solution)/shard_map/retro/pallas_call | solution.py:447
  141.2 1.9 %copy.17 = bf16[256,1024]{1,0:T(8,128)(2,1)} copy(bf16[256,1024]{1,0:T(8,128)(2,1)} %get-tuple-element.8) | data formatting | bytes 1048576
  143.1 1.5 copy.18
  144.6 1.4 copy.19
  145.9 1.4 copy.20
  (2 shorter events, 0.0 us)

commit v3 on v2

--- a/solution.py
+++ b/solution.py
@@ -1,5 +1,3 @@
-import functools
-
 import jax
 import jax.numpy as jnp
 from jax import lax
@@ -17,14 +15,13 @@
 INNER = 1024
 D = 2048
 CHIPS = 64
-PARTS = ((0, 384), (384, 384), (768, 256))
-WIDTHS = tuple(w for _, w in PARTS) * 2
 LEVELS = 6
-CHUNKS = ((0, 384), (384, 256), (640, 256))
+OFFSETS = (0, 32, 48)
+TURNS = (0, 1, 2, 3, 4, 5, 0, 3, 0, 1, 2, 3, 4, 5, 1, 4)
+CHUNKS = ((0, 384), (384, 384), (768, 128))
 DP_ORDER = (1, 4, 3, 12, 2, 8, 5, 15, 7, 13, 6, 9, 11, 14, 10)
 WEIGHT_ROWS = (256, 112, 112)
 WEIGHT_CUTS = (128, 64, 48)
-OFFSETS = (0, 32, 48, 56, 60, 62)
 NT_DIMS = (((1,), (1,)), ((), ()))
 MESH = pl.DeviceIdType.MESH
 
@@ -69,23 +66,23 @@
 
 
 def whole_kernel(
-    id_row, tok_in, cot_in, cache_in, wq_in, wk_in, wv_in, ctx, gq, gk, gv, *scratch
+    own_ids, tok_in, cot_in, cache_in, wq_in, wk_in, wv_in, ctx_out, grads, *scratch
 ):
     it = iter(scratch)
 
     def take(n=None):
         return next(it) if n is None else tuple(next(it) for _ in range(n))
 
-    ids_shard, id_group, ids_dp, asked_v, slots_v, asked_s, slots_s = take(7)
+    id_row, ids_shard, id_group, ids_dp, asked_v, slots_v, asked_s, slots_s = take(8)
     cache, tok, cot = take(3)
     weights = take(3)
     wq, wk, wv = weights
     outgoing, replies, chosen = take(3), take(3), take(3)
     lat = take()
-    normed, q, kb, vb, qg, kg, vg, lat_t = take(8)
-    xs, crecv, acc, snd, rcv = take(6), take(6), take(6), take(6), take(6)
+    normed, normed_t, q, kb, vb, qg, kg, vg, lat_t, ctx = take(10)
+    xs, crecv, acc, snd, rcv = take(5)
     local_sem, id_send, id_recv, gid_send, gid_recv, w_send, w_recv = take(7)
-    dp_send, dp_recv, sh_send, sh_recv, csem, send_sem, recv_sem = take(7)
+    dp_send, dp_recv, sh_send, sh_recv, send_sem, recv_sem = take(6)
 
     dp = lax.axis_index("dp")
     shard = lax.axis_index("shard")
@@ -130,7 +127,12 @@
 
     pl.semaphore_wait(barrier, 22)
 
-    ids_shard[shard] = id_row[...]
+    row_lane = lax.broadcasted_iota(jnp.int32, (8, 128), 1)
+    own_row = jnp.zeros((8, 128), jnp.int32)
+    for k in range(8):
+        own_row = jnp.where(row_lane == shard * 8 + k, own_ids[k // 2, k % 2], own_row)
+    id_row[...] = own_row
+    ids_shard[shard] = own_row
     asks = [
         send(id_row, ids_shard.at[shard], id_send.at[r], id_recv.at[r], (dp, shard ^ r))
         for r in range(1, 8)
@@ -228,6 +230,13 @@
         inverse = lax.rsqrt(jnp.mean(t * t, axis=-1, keepdims=True) + 1e-06)
         normed[rows, :] = (t * inverse).astype(jnp.bfloat16)
 
+    eye_wide = one_hot(256, 256, lambda r, c: r == c)
+
+    @pl.loop(0, 8)
+    def _(i):
+        cols = pl.ds(pl.multiple_of(i * 256, 256), 256)
+        normed_t[cols, :] = nt_dot(eye_wide, normed[:, cols]).astype(jnp.bfloat16)
+
     spread = []
 
     def hand_on(c):
@@ -274,9 +283,28 @@
         cols = pl.ds(pl.multiple_of(i * 256, 256), 256)
         q[:, cols] = (nn_dot(normed[...], wq[:, cols]) * scale).astype(jnp.bfloat16)
 
+    def turn_latents(b):
+        at, width = ((0, 256), (128, 384), (384, 384), (640, 256))[b]
+        pick = one_hot(
+            256,
+            width,
+            lambda r, c: (c + at == 224 * b + 7 * (r >> 3) + (r & 7)) & ((r & 7) < 7),
+        )
+        for n in range(4):
+            block = lat[2 * n : 2 * n + 2, :, :, at : at + width].reshape(256, width)
+            lat_t[256 * b : 256 * b + 256, 256 * n : 256 * n + 256] = nt_dot(pick, block).astype(
+                jnp.bfloat16
+            )
+
+    early = list(spread)
     hand_on(2)
-    for copy in spread:
+    for copy in early:
         copy.wait_recv()
+    for b in range(3):
+        turn_latents(b)
+    for copy in spread[len(early) :]:
+        copy.wait_recv()
+    turn_latents(3)
 
     eye = one_hot(128, 128, lambda r, c: r == c)
     zero = jnp.zeros((SPAN, HEAD_DIM), jnp.bfloat16)
@@ -320,141 +348,197 @@
             qg[trows, at:mid] = qg2[:SPAN, :HEAD_DIM]
             qg[trows, mid:end] = qg2[SPAN:, HEAD_DIM:]
 
-    partners = []
-    for d in range(LEVELS):
-        high = d % 2 == 0
-        if d < 2:
-            partners.append((flip(z, high) * 4 + x, shard))
-        elif d < 4:
-            partners.append((z * 4 + flip(x, high), shard))
-        else:
-            partners.append((dp, flip(y, high) * 2 + core))
+    ctx_copy = pltpu.make_async_copy(ctx, ctx_out, local_sem.at[8])
+    ctx_copy.start()
+
+    def across(dims):
+        pz, px, py = z, x, y
+        for d in dims:
+            if d < 2:
+                pz = flip(pz, d % 2 == 0)
+            elif d < 4:
+                px = flip(px, d % 2 == 0)
+            else:
+                py = flip(py, d % 2 == 0)
+        return (pz * 4 + px, py * 2 + core)
+
     here = place(z * 16 + x * 4 + y, 0)
-    coming = [None] * 6
-    base = [0] * 6
-    root = [0] * 6
-
-    def to_other_core(p):
-        coming[p] = send(xs[p].at[1 - core], crecv[p], csem.at[0, p], csem.at[1, p], other)
-
-    def halve(k, p):
-        half = CHIPS >> (k + 1)
-        step = min(half, 8)
-        d = (p + k) % LEVELS
-        bit = (here >> (LEVELS - 1 - d)) & 1
-        away = base[p] + (1 - bit) * half
-        keep = base[p] + bit * half
-        coming[p].wait_recv()
-        if k == 0:
-            root[p] = keep
+    coming = [None] * 16
+    base = [0] * 16
+    root = [0] * 16
+
+    def to_other_core(t):
+        coming[t] = send(
+            xs.at[t, 1 - core], crecv.at[t], send_sem.at[0, t], recv_sem.at[0, t], other
+        )
+
+    def totals(k, t):
+        step = min(CHIPS >> (k + 1), 16)
 
         def summed(at):
             where = pl.ds(at, step)
             if k == 0:
-                return xs[p][core, where].astype(jnp.float32) + crecv[p][where].astype(jnp.float32)
-            back = pl.ds(OFFSETS[k - 1] + at - base[p], step)
-            return acc[p][pl.ds(at - root[p], step)] + rcv[p][back].astype(jnp.float32)
+                return xs[t, core, where].astype(jnp.float32) + crecv[t, where].astype(jnp.float32)
+            back = pl.ds(OFFSETS[k - 1] + at - base[t], step)
+            return acc[t, pl.ds(at - root[t], step)] + rcv[t, back].astype(jnp.float32)
+
+        return summed, step
+
+    def halve(k, t):
+        half = CHIPS >> (k + 1)
+        d = (TURNS[t] + k) % LEVELS
+        bit = (here >> (LEVELS - 1 - d)) & 1
+        away = base[t] + (1 - bit) * half
+        keep = base[t] + bit * half
+        coming[t].wait_recv()
+        if k == 0:
+            root[t] = keep
+        summed, step = totals(k, t)
 
         @pl.loop(0, half // step)
         def _(i):
-            snd[p][pl.ds(OFFSETS[k] + i * step, step)] = summed(away + i * step).astype(
+            snd[t, pl.ds(OFFSETS[k] + i * step, step)] = summed(away + i * step).astype(
                 jnp.bfloat16
             )
 
         span = pl.ds(OFFSETS[k], half)
         copy = send(
-            snd[p].at[span], rcv[p].at[span], send_sem.at[k, p], recv_sem.at[k, p], partners[d]
+            snd.at[t, span],
+            rcv.at[t, span],
+            send_sem.at[1 + k, t],
+            recv_sem.at[1 + k, t],
+            across((d,)),
         )
 
         @pl.loop(0, half // step)
         def _(i):
-            acc[p][pl.ds(keep - root[p] + i * step, step)] = summed(keep + i * step)
-
-        base[p] = keep
-        coming[p] = copy
-
-    eye_wide = one_hot(256, 256, lambda r, c: r == c)
-
-    @pl.loop(0, 8)
-    def _(i):
-        cols = pl.ds(pl.multiple_of(i * 256, 256), 256)
-        turned = nt_dot(eye_wide, normed[:, cols]).astype(jnp.bfloat16)
-        for p, (at, width) in enumerate(PARTS):
-            r = nn_dot(turned, qg[:, at : at + width]).astype(jnp.bfloat16)
-            for j in range(16):
-                xs[p][j & 1, place(8 * i + (j >> 1), p)] = r[16 * j : 16 * j + 16, :]
-
-    for p in range(3):
-        to_other_core(p)
-
-    for b, (at, width) in enumerate(((0, 256), (128, 384), (384, 384), (640, 256))):
-        pick = one_hot(
-            256,
-            width,
-            lambda r, c: (c + at == 224 * b + 7 * (r >> 3) + (r & 7)) & ((r & 7) < 7),
+            acc[t, pl.ds(keep - root[t] + i * step, step)] = summed(keep + i * step)
+
+        base[t] = keep
+        coming[t] = copy
+
+    last = {}
+
+    def exchange_rest(t):
+        coming[t].wait_recv()
+        whole = acc[t, pl.ds(base[t] - root[t], 8)] + rcv[t, pl.ds(OFFSETS[2], 8)].astype(
+            jnp.float32
         )
-        for n in range(4):
-            block = lat[2 * n : 2 * n + 2, :, :, at : at + width].reshape(256, width)
-            lat_t[256 * b : 256 * b + 256, 256 * n : 256 * n + 256] = nt_dot(pick, block).astype(
-                jnp.bfloat16
+        acc[t, pl.ds(base[t] - root[t], 8)] = whole
+        snd[t, pl.ds(56, 8)] = whole.astype(jnp.bfloat16)
+        own = place(z * 16 + x * 4 + y, TURNS[t]) & 7
+        last[t] = []
+        for m in (4, 2, 1, 6, 5, 3, 7):
+            dims = [(TURNS[t] + 3 + e) % LEVELS for e in range(3) if m & (4 >> e)]
+            last[t].append(
+                send(
+                    snd.at[t, 56 + (own ^ m)],
+                    rcv.at[t, 56 + m],
+                    send_sem.at[4 + m, t],
+                    recv_sem.at[4 + m, t],
+                    across(dims),
+                )
             )
 
-    for p in range(3):
-        halve(0, p)
-
-    for p, (at, width) in enumerate(PARTS):
+    def finish(t):
+        for copy in last[t]:
+            copy.wait_recv()
+        own = place(z * 16 + x * 4 + y, TURNS[t]) & 7
+        total = acc[t, base[t] - root[t] + own]
+        for m in range(1, 8):
+            total = total + rcv[t, 56 + m].astype(jnp.float32)
+        at = 128 * (t % 8)
+        grads[16 * (t // 8) : 16 * (t // 8) + 16, at : at + 128] = total
+
+    for n in range(4):
 
         @pl.loop(0, 4)
+        def _(i):
+            turned = normed_t[pl.ds(pl.multiple_of(i * 512, 512), 512), :]
+            r = nn_dot(turned, qg[:, 256 * n : 256 * n + 256]).astype(jnp.bfloat16)
+            for j in range(32):
+                for e in range(2):
+                    t = 2 * n + e
+                    xs[t, j & 1, place(16 * i + (j >> 1), TURNS[t])] = r[
+                        16 * j : 16 * j + 16, 128 * e : 128 * e + 128
+                    ]
+
+        to_other_core(2 * n)
+        to_other_core(2 * n + 1)
+
+    plan = (
+        ((0, 0), (0, 1), (0, 2), (0, 3)),
+        ((0, 4), (0, 5), (0, 6), (0, 7)),
+        ((0, 8), (0, 9), (1, 0), (1, 1), (1, 2), (1, 3)),
+        (
+            *((0, t) for t in (10, 11)),
+            *((1, t) for t in (4, 5, 6, 7)),
+            *((0, t) for t in (12, 13)),
+            *((2, t) for t in (0, 1, 2, 3)),
+            *((0, t) for t in (14, 15)),
+            *((1, t) for t in (8, 9, 10, 11)),
+            *((2, t) for t in (4, 5, 6, 7)),
+            *((3, t) for t in (0, 1, 2, 3)),
+            *((1, t) for t in (12, 13, 14, 15)),
+            *((2, t) for t in (8, 9, 10, 11)),
+            *((3, t) for t in (4, 5, 6, 7)),
+            *((2, t) for t in (12, 13, 14, 15)),
+            *((3, t) for t in range(8, 16)),
+        ),
+    )
+    for n in range(4):
+
+        @pl.loop(0, 2)
         def _(b):
-            turned = lat_t[pl.ds(pl.multiple_of(b * 256, 256), 256), :]
-            rk = nn_dot(turned, kg[:, at : at + width])
-            rv = nn_dot(turned, vg[:, at : at + width])
-            for j in range(32):
+            turned = lat_t[pl.ds(pl.multiple_of(b * 512, 512), 512), :]
+            rk = nn_dot(turned, kg[:, 256 * n : 256 * n + 256])
+            rv = nn_dot(turned, vg[:, 256 * n : 256 * n + 256])
+            for j in range(64):
                 both = jnp.concatenate([rk[8 * j : 8 * j + 8], rv[8 * j : 8 * j + 8]], axis=0)
-                xs[3 + p][j & 1, place(16 * b + (j >> 1), 3 + p)] = both.astype(jnp.bfloat16)
-
-        to_other_core(3 + p)
-
-    for p in range(3, 6):
-        halve(0, p)
-    for k in range(1, LEVELS):
-        for p in range(6):
-            halve(k, p)
-    for p in range(6):
-        coming[p].wait_recv()
-        total = acc[p][base[p] - root[p]] + rcv[p][OFFSETS[5]].astype(jnp.float32)
-        at, width = PARTS[p % 3]
-        if p < 3:
-            gq[:, at : at + width] = total
-        else:
-            gk[:, at : at + width] = total[0:7]
-            gv[:, at : at + width] = total[8:15]
+                both = both.astype(jnp.bfloat16)
+                for e in range(2):
+                    t = 8 + 2 * n + e
+                    xs[t, j & 1, place(32 * b + (j >> 1), TURNS[t])] = both[
+                        :, 128 * e : 128 * e + 128
+                    ]
+
+        to_other_core(8 + 2 * n)
+        to_other_core(9 + 2 * n)
+        for k, t in plan[n]:
+            if k < 3:
+                halve(k, t)
+            else:
+                exchange_rest(t)
+    for t in range(16):
+        finish(t)
+    ctx_copy.wait()
     for copy in pending:
         copy.wait_send()
 
 
+def emit_kernel(ctx, grads, ctx_out, gq, gk, gv):
+    ctx_out[...] = ctx[...]
+    gq[...] = grads[0:16]
+    gk[...] = grads[16:23]
+    gv[...] = grads[24:31]
+
+
 def body(tokens, ctx_cotangent, latent_cache, nbr_ids, w_query, w_key, w_value):
-    lane = jnp.arange(128, dtype=jnp.int32)
-    id_row = jnp.where(
-        lane // 8 == lax.axis_index("shard"), jnp.tile(nbr_ids.reshape(-1), 16), 0
-    )
-    id_row = jnp.broadcast_to(id_row[None], (8, 128))
     f32, bf, i32 = jnp.float32, jnp.bfloat16, jnp.int32
     vmem = pl.BlockSpec(memory_space=pltpu.VMEM)
     hbm = pl.BlockSpec(memory_space=pl.ANY)
     dma = pltpu.SemaphoreType.DMA
     widths = [w for _, w in CHUNKS]
-    return pl.pallas_call(
+    context, grads = pl.pallas_call(
         whole_kernel,
         out_shape=(
             jax.ShapeDtypeStruct((256, INNER), bf),
-            jax.ShapeDtypeStruct((16, INNER), f32),
-            jax.ShapeDtypeStruct((7, INNER), f32),
-            jax.ShapeDtypeStruct((7, INNER), f32),
+            jax.ShapeDtypeStruct((32, INNER), f32),
         ),
-        in_specs=[vmem] + [hbm] * 6,
-        out_specs=(vmem,) * 4,
+        in_specs=[pl.BlockSpec(memory_space=pltpu.SMEM)] + [hbm] * 6,
+        out_specs=(hbm, vmem),
         scratch_shapes=[
+            pltpu.VMEM((8, 128), i32),
             pltpu.VMEM((8, 8, 128), i32),
             pltpu.VMEM((8, 128), i32),
             pltpu.VMEM((16, 8, 128), i32),
@@ -473,6 +557,7 @@
             *(pltpu.VMEM((8, 8, 16, w), bf) for w in widths),
             pltpu.VMEM((8, 8, 16, LAT), bf),
             pltpu.VMEM((256, D), bf),
+            pltpu.VMEM((D, 256), bf),
             pltpu.VMEM((256, INNER), bf),
             pltpu.VMEM((256, INNER), bf),
             pltpu.VMEM((256, INNER), bf),
@@ -480,12 +565,13 @@
             pltpu.VMEM((1024, INNER), bf),
             pltpu.VMEM((1024, INNER), bf),
             pltpu.VMEM((1024, 1024), bf),
-            *(pltpu.VMEM((2, CHIPS, 16, w), bf) for w in WIDTHS),
-            *(pltpu.VMEM((CHIPS, 16, w), bf) for w in WIDTHS),
-            *(pltpu.VMEM((CHIPS // 2, 16, w), f32) for w in WIDTHS),
-            *(pltpu.VMEM((CHIPS, 16, w), bf) for w in WIDTHS),
-            *(pltpu.VMEM((CHIPS, 16, w), bf) for w in WIDTHS),
-            dma((8,)),
+            pltpu.VMEM((256, INNER), bf),
+            pltpu.VMEM((16, 2, CHIPS, 16, 128), bf),
+            pltpu.VMEM((16, CHIPS, 16, 128), bf),
+            pltpu.VMEM((16, CHIPS // 2, 16, 128), f32),
+            pltpu.VMEM((16, CHIPS, 16, 128), bf),
+            pltpu.VMEM((16, CHIPS, 16, 128), bf),
+            dma((9,)),
             dma((8,)),
             dma((8,)),
             dma((16,)),
@@ -496,16 +582,15 @@
             dma((3, 16)),
             dma((3, 8)),
             dma((3, 8)),
-            dma((2, 6)),
-            dma((LEVELS, 6)),
-            dma((LEVELS, 6)),
+            dma((12, 16)),
+            dma((12, 16)),
         ],
         compiler_params=pltpu.CompilerParams(
             collective_id=1, has_side_effects=True, vmem_limit_bytes=67043328
         ),
         name="retro",
     )(
-        id_row,
+        nbr_ids,
         tokens,
         ctx_cotangent,
         latent_cache,
@@ -513,6 +598,18 @@
         w_key,
         w_value,
     )
+    return pl.pallas_call(
+        emit_kernel,
+        out_shape=(
+            jax.ShapeDtypeStruct((256, INNER), bf),
+            jax.ShapeDtypeStruct((16, INNER), f32),
+            jax.ShapeDtypeStruct((7, INNER), f32),
+            jax.ShapeDtypeStruct((7, INNER), f32),
+        ),
+        in_specs=[vmem] * 2,
+        out_specs=(vmem,) * 4,
+        name="emit",
+    )(context, grads)
 
 
 def solution(mesh):

time: 148 us -> 135 us (0.912)
  Pallas kernels: 139 us -> 132 us
  local copies, waits for them, and re-layouts: 7.63 us -> 1.34 us
    pallas_call x1, Pallas kernels: 139 us -> 131 us  [body(): pl.pallas_call(whole_kernel, out_shape=(jax.ShapeDtypeStruct((256, INNER)...]
    unnamed x5 -> x1, local copies, waits for them, and re-layouts: 6.86 us -> 1.34 us
    pallas_call x0 -> x1, Pallas kernels: none -> 1.91 us  [body(): pl.pallas_call(emit_kernel, out_shape=(jax.ShapeDtypeStruct((256, INNER),...]
where the time goes in v3:
time: 135 us; the launch traced here: 134 us
  Pallas kernels  132 us (98%)
    pallas_call x1, Pallas kernels, body(): pl.pallas_call(whole_kernel, out_shape=(jax.ShapeDtypeStruct((256, INNER)...  131 us

profile of v3, /device:TPU:0, one launch (start us, length us, event | category | flops | bytes accessed | tf_op | source)
XLA Modules:
  0.0 134.4 jit_solution(13512079458673501187)
XLA Ops:
  0.6 1.3 copy.11.own_ids
  2.0 130.5 %retro.1 = (bf16[256,1024]{1,0:T(8,128)(2,1)}, f32[32,1024]{1,0:T(8,128)}) custom-call(s32[4,2]{1,0:T(4,128)} %copy.11.own_ids, bf16[256,2048]{1,0:T(8,128)(2,1)} %tok_in.1, bf16[256,1024]{1,0:T(8,128)(2,1)} %cot_in.1, bf16[128,16,896]{2,1,0:T(8,128)(2,1)} %cache_in.1, bf16[256,1024]{1,0:T(8,128)(2,1)} %wq_in.1, bf16[112,1024]{1,0:T(8,128)(2,1)} %wk_in.1, ...), custom_call_target="tpu_custom_call" | custom-call | tf_op jit(solution)/shard_map/retro/pallas_call | solution.py:532
  132.5 1.9 %emit.1 = (bf16[256,1024]{1,0:T(8,128)(2,1)}, f32[16,1024]{1,0:T(8,128)}, f32[7,1024]{1,0:T(8,128)}, f32[7,1024]{1,0:T(8,128)}) custom-call(bf16[256,1024]{1,0:T(8,128)(2,1)} %get-tuple-element.6.ctx, f32[32,1024]{1,0:T(8,128)} %get-tuple-element.7.grads), custom_call_target="tpu_custom_call" | custom-call | tf_op jit(solution)/shard_map/emit/pallas_call | solution.py:601

commit v4 on v3

--- a/solution.py
+++ b/solution.py
@@ -17,7 +17,7 @@
 CHIPS = 64
 LEVELS = 6
 OFFSETS = (0, 32, 48)
-TURNS = (0, 1, 2, 3, 4, 5, 0, 3, 0, 1, 2, 3, 4, 5, 1, 4)
+TURNS = (0, 1, 4, 5, 2, 3, 0, 1, 2, 3, 0, 1, 4, 5, 2, 3)
 CHUNKS = ((0, 384), (384, 384), (768, 128))
 DP_ORDER = (1, 4, 3, 12, 2, 8, 5, 15, 7, 13, 6, 9, 11, 14, 10)
 WEIGHT_ROWS = (256, 112, 112)
@@ -79,8 +79,8 @@
     wq, wk, wv = weights
     outgoing, replies, chosen = take(3), take(3), take(3)
     lat = take()
-    normed, normed_t, q, kb, vb, qg, kg, vg, lat_t, ctx = take(10)
-    xs, crecv, acc, snd, rcv = take(5)
+    normed, normed_t, q, qg, kg, vg, lat_t, ctx = take(8)
+    xs, crecv, acc, snd, rcv, value_part = take(6)
     local_sem, id_send, id_recv, gid_send, gid_recv, w_send, w_recv = take(7)
     dp_send, dp_recv, sh_send, sh_recv, send_sem, recv_sem = take(6)
 
@@ -130,7 +130,7 @@
     row_lane = lax.broadcasted_iota(jnp.int32, (8, 128), 1)
     own_row = jnp.zeros((8, 128), jnp.int32)
     for k in range(8):
-        own_row = jnp.where(row_lane == shard * 8 + k, own_ids[k // 2, k % 2], own_row)
+        own_row = jnp.where(row_lane == shard * 8 + k, own_ids[k % 2, k // 2], own_row)
     id_row[...] = own_row
     ids_shard[shard] = own_row
     asks = [
@@ -261,6 +261,25 @@
             )
         lat[:, shard, :, at : at + width] = chosen[c][shard]
 
+    def project(c):
+        at, width = CHUNKS[c]
+        for copy in spread[7 * c : 7 * c + 7]:
+            copy.wait_recv()
+
+        @pl.loop(0, CH_DEV)
+        def _(n):
+            block = lat[pl.ds(2 * n, 2), :, :, at : at + width].reshape(256, width)
+            rows = pl.ds(pl.multiple_of((n & 1) * 16, 16), 16)
+            for w, total in ((wk, acc), (wv, value_part)):
+                for j in range(0, 8, 2):
+                    r = nn_dot(block, w[at : at + width, 128 * j : 128 * j + 256])
+                    for e in range(2):
+                        tile = r[:, 128 * e : 128 * e + 128].reshape(16, 16, 128)
+                        index = (n >> 1) * 8 + j + e
+                        if c > 0:
+                            tile = tile + total[index, rows]
+                        total[index, rows] = tile
+
     arrived(0)
     send_weights(3, down, (dp, up * 2 + core), 0)
     send_weights(5, down, other)
@@ -296,13 +315,12 @@
                 jnp.bfloat16
             )
 
-    early = list(spread)
+    project(0)
     hand_on(2)
-    for copy in early:
-        copy.wait_recv()
+    project(1)
     for b in range(3):
         turn_latents(b)
-    for copy in spread[len(early) :]:
+    for copy in spread[14:]:
         copy.wait_recv()
     turn_latents(3)
 
@@ -316,19 +334,23 @@
             [jnp.concatenate([a, zero], axis=1), jnp.concatenate([zero, b], axis=1)], axis=0
         )
 
-    @pl.loop(0, CH_DEV)
-    def _(c):
-        rows = pl.ds(pl.multiple_of(c * 256, 256), 256)
-        trows = pl.ds(pl.multiple_of(c * SPAN, SPAN), SPAN)
-        block = lat[pl.ds(2 * c, 2)].reshape(256, LAT)
-        for at in range(0, INNER, 256):
-            kb[:, at : at + 256] = nn_dot(block, wk[:, at : at + 256]).astype(jnp.bfloat16)
-            vb[:, at : at + 256] = nn_dot(block, wv[:, at : at + 256]).astype(jnp.bfloat16)
-        for at in range(0, INNER, 256):
-            mid = at + HEAD_DIM
-            end = at + 256
-            kp = kb[:, at:end]
-            vp = vb[:, at:end]
+    def project_last(w, total, c, at):
+        block = lat[2 * c : 2 * c + 2, :, :, 768:LAT].reshape(256, 128)
+        r = nn_dot(block, w[768:LAT, at : at + 256])
+        tiles = [
+            total[(c >> 1) * 8 + at // 128 + e, 16 * (c & 1) : 16 * (c & 1) + 16].reshape(256, 128)
+            for e in range(2)
+        ]
+        return (jnp.concatenate(tiles, axis=1) + r).astype(jnp.bfloat16)
+
+    def attend(at):
+        mid = at + HEAD_DIM
+        end = at + 256
+        for c in range(CH_DEV):
+            rows = slice(256 * c, 256 * c + 256)
+            trows = slice(SPAN * c, SPAN * c + SPAN)
+            kp = project_last(wk, acc, c, at)
+            vp = project_last(wv, value_part, c, at)
             q2 = diagonal(q, trows, at)
             g2 = diagonal(cot, trows, at)
             scores = nt_dot(kp, q2)
@@ -339,17 +361,14 @@
             c2 = nn_dot(prob_r, vp).astype(jnp.bfloat16)
             ctx[trows, at:mid] = c2[:SPAN, :HEAD_DIM]
             ctx[trows, mid:end] = c2[SPAN:, HEAD_DIM:]
-            vg[rows, at:end] = nn_dot(prob_t, g2).astype(jnp.bfloat16)
+            vg[rows, :] = nn_dot(prob_t, g2).astype(jnp.bfloat16)
             pg = nt_dot(vp, g2)
             sg_t = (prob * (pg - jnp.sum(prob * pg, axis=0, keepdims=True))).astype(jnp.bfloat16)
-            kg[rows, at:end] = nn_dot(sg_t, q2).astype(jnp.bfloat16)
+            kg[rows, :] = nn_dot(sg_t, q2).astype(jnp.bfloat16)
             sg = nt_dot(eye, sg_t).astype(jnp.bfloat16)
             qg2 = (nn_dot(sg, kp) * scale).astype(jnp.bfloat16)
-            qg[trows, at:mid] = qg2[:SPAN, :HEAD_DIM]
-            qg[trows, mid:end] = qg2[SPAN:, HEAD_DIM:]
-
-    ctx_copy = pltpu.make_async_copy(ctx, ctx_out, local_sem.at[8])
-    ctx_copy.start()
+            qg[trows, :HEAD_DIM] = qg2[:SPAN, :HEAD_DIM]
+            qg[trows, HEAD_DIM:] = qg2[SPAN:, HEAD_DIM:]
 
     def across(dims):
         pz, px, py = z, x, y
@@ -450,12 +469,11 @@
         at = 128 * (t % 8)
         grads[16 * (t // 8) : 16 * (t // 8) + 16, at : at + 128] = total
 
-    for n in range(4):
-
+    def query_sums(n):
         @pl.loop(0, 4)
         def _(i):
             turned = normed_t[pl.ds(pl.multiple_of(i * 512, 512), 512), :]
-            r = nn_dot(turned, qg[:, 256 * n : 256 * n + 256]).astype(jnp.bfloat16)
+            r = nn_dot(turned, qg[...]).astype(jnp.bfloat16)
             for j in range(32):
                 for e in range(2):
                     t = 2 * n + e
@@ -466,33 +484,12 @@
         to_other_core(2 * n)
         to_other_core(2 * n + 1)
 
-    plan = (
-        ((0, 0), (0, 1), (0, 2), (0, 3)),
-        ((0, 4), (0, 5), (0, 6), (0, 7)),
-        ((0, 8), (0, 9), (1, 0), (1, 1), (1, 2), (1, 3)),
-        (
-            *((0, t) for t in (10, 11)),
-            *((1, t) for t in (4, 5, 6, 7)),
-            *((0, t) for t in (12, 13)),
-            *((2, t) for t in (0, 1, 2, 3)),
-            *((0, t) for t in (14, 15)),
-            *((1, t) for t in (8, 9, 10, 11)),
-            *((2, t) for t in (4, 5, 6, 7)),
-            *((3, t) for t in (0, 1, 2, 3)),
-            *((1, t) for t in (12, 13, 14, 15)),
-            *((2, t) for t in (8, 9, 10, 11)),
-            *((3, t) for t in (4, 5, 6, 7)),
-            *((2, t) for t in (12, 13, 14, 15)),
-            *((3, t) for t in range(8, 16)),
-        ),
-    )
-    for n in range(4):
-
+    def latent_sums(n):
         @pl.loop(0, 2)
         def _(b):
             turned = lat_t[pl.ds(pl.multiple_of(b * 512, 512), 512), :]
-            rk = nn_dot(turned, kg[:, 256 * n : 256 * n + 256])
-            rv = nn_dot(turned, vg[:, 256 * n : 256 * n + 256])
+            rk = nn_dot(turned, kg[...])
+            rv = nn_dot(turned, vg[...])
             for j in range(64):
                 both = jnp.concatenate([rk[8 * j : 8 * j + 8], rv[8 * j : 8 * j + 8]], axis=0)
                 both = both.astype(jnp.bfloat16)
@@ -504,11 +501,27 @@
 
         to_other_core(8 + 2 * n)
         to_other_core(9 + 2 * n)
-        for k, t in plan[n]:
+
+    def reduce(k, n):
+        for t in (2 * n, 2 * n + 1, 8 + 2 * n, 9 + 2 * n):
             if k < 3:
                 halve(k, t)
             else:
                 exchange_rest(t)
+
+    for n in range(4):
+        attend(256 * n)
+        if n == 3:
+            ctx_copy = pltpu.make_async_copy(ctx, ctx_out, local_sem.at[8])
+            ctx_copy.start()
+        if n > 0:
+            reduce(0, n - 1)
+        query_sums(n)
+        latent_sums(n)
+        for k in range(1, n):
+            reduce(k, n - 1 - k)
+    for k, n in ((0, 3), (1, 2), (2, 1), (3, 0), (1, 3), (2, 2), (3, 1), (2, 3), (3, 2), (3, 3)):
+        reduce(k, n)
     for t in range(16):
         finish(t)
     ctx_copy.wait()
@@ -559,11 +572,9 @@
             pltpu.VMEM((256, D), bf),
             pltpu.VMEM((D, 256), bf),
             pltpu.VMEM((256, INNER), bf),
-            pltpu.VMEM((256, INNER), bf),
-            pltpu.VMEM((256, INNER), bf),
-            pltpu.VMEM((256, INNER), bf),
-            pltpu.VMEM((1024, INNER), bf),
-            pltpu.VMEM((1024, INNER), bf),
+            pltpu.VMEM((256, 256), bf),
+            pltpu.VMEM((1024, 256), bf),
+            pltpu.VMEM((1024, 256), bf),
             pltpu.VMEM((1024, 1024), bf),
             pltpu.VMEM((256, INNER), bf),
             pltpu.VMEM((16, 2, CHIPS, 16, 128), bf),
@@ -571,6 +582,7 @@
             pltpu.VMEM((16, CHIPS // 2, 16, 128), f32),
             pltpu.VMEM((16, CHIPS, 16, 128), bf),
             pltpu.VMEM((16, CHIPS, 16, 128), bf),
+            pltpu.VMEM((16, CHIPS // 2, 16, 128), f32),
             dma((9,)),
             dma((8,)),
             dma((8,)),
@@ -590,7 +602,7 @@
         ),
         name="retro",
     )(
-        nbr_ids,
+        nbr_ids.T,
         tokens,
         ctx_cotangent,
         latent_cache,

time: 135 us -> 128 us (0.948)
  Pallas kernels: 132 us -> 127 us
    pallas_call x1, Pallas kernels: 131 us -> 125 us  [body(): pl.pallas_call(whole_kernel, out_shape=(jax.ShapeDtypeStruct((256, INNER)...]
where the time goes in v4:
time: 128 us; the launch traced here: 127 us
  Pallas kernels  127 us (99%)
    pallas_call x1, Pallas kernels, body(): pl.pallas_call(whole_kernel, out_shape=(jax.ShapeDtypeStruct((256, INNER)...  125 us

profile of v4, /device:TPU:0, one launch (start us, length us, event | category | flops | bytes accessed | tf_op | source)
XLA Modules:
  0.0 127.4 jit_solution(3716366006901117212)
XLA Ops:
  0.6 124.9 %retro.1 = (bf16[256,1024]{1,0:T(8,128)(2,1)}, f32[32,1024]{1,0:T(8,128)}) custom-call(s32[2,4]{1,0:T(2,128)} %bitcast.1, bf16[256,2048]{1,0:T(8,128)(2,1)} %tok_in.1, bf16[256,1024]{1,0:T(8,128)(2,1)} %cot_in.1, bf16[128,16,896]{2,1,0:T(8,128)(2,1)} %cache_in.1, bf16[256,1024]{1,0:T(8,128)(2,1)} %wq_in.1, bf16[112,1024]{1,0:T(8,128)(2,1)} %wk_in.1, ...), custom_call_target="tpu_custom_call" | custom-call | tf_op jit(solution)/shard_map/retro/pallas_call | solution.py:545
  125.5 1.9 %emit.1 = (bf16[256,1024]{1,0:T(8,128)(2,1)}, f32[16,1024]{1,0:T(8,128)}, f32[7,1024]{1,0:T(8,128)}, f32[7,1024]{1,0:T(8,128)}) custom-call(bf16[256,1024]{1,0:T(8,128)(2,1)} %get-tuple-element.6.ctx, f32[32,1024]{1,0:T(8,128)} %get-tuple-element.7.grads), custom_call_target="tpu_custom_call" | custom-call | tf_op jit(solution)/shard_map/emit/pallas_call | solution.py:613

commit v5 on v4

--- a/solution.py
+++ b/solution.py
@@ -15,10 +15,7 @@
 INNER = 1024
 D = 2048
 CHIPS = 64
-LEVELS = 6
-OFFSETS = (0, 32, 48)
-TURNS = (0, 1, 4, 5, 2, 3, 0, 1, 2, 3, 0, 1, 4, 5, 2, 3)
-CHUNKS = ((0, 384), (384, 384), (768, 128))
+CHUNKS = ((0, 384), (384, 128), (512, 128), (640, 128), (768, 128))
 DP_ORDER = (1, 4, 3, 12, 2, 8, 5, 15, 7, 13, 6, 9, 11, 14, 10)
 WEIGHT_ROWS = (256, 112, 112)
 WEIGHT_CUTS = (128, 64, 48)
@@ -34,9 +31,11 @@
     return jnp.dot(a, b, preferred_element_type=jnp.float32)
 
 
-def place(chip, part):
+def place(chip, low_first):
     code = chip ^ ((chip >> 1) & 21)
-    return ((code << part) | (code >> (LEVELS - part))) & (CHIPS - 1)
+    high = ((code >> 3) & 4) | ((code >> 2) & 2) | ((code >> 1) & 1)
+    low = ((code >> 2) & 4) | ((code >> 1) & 2) | (code & 1)
+    return (low << 3) | high if low_first else (high << 3) | low
 
 
 def one_hot(rows, columns, wanted):
@@ -77,7 +76,7 @@
     cache, tok, cot = take(3)
     weights = take(3)
     wq, wk, wv = weights
-    outgoing, replies, chosen = take(3), take(3), take(3)
+    outgoing, replies, chosen = take(5), take(5), take(5)
     lat = take()
     normed, normed_t, q, qg, kg, vg, lat_t, ctx = take(8)
     xs, crecv, acc, snd, rcv, value_part = take(6)
@@ -203,7 +202,7 @@
                 outgoing[c][g, j] = cache[row, :, at : at + width]
 
     fetches = []
-    for c in range(3):
+    for c in range(len(CHUNKS)):
         own = pl.ds(pl.multiple_of(dp * 8, 8), 8)
         fetches.append(
             [
@@ -217,7 +216,7 @@
                 for r in DP_ORDER
             ]
         )
-    for c in range(3):
+    for c in range(len(CHUNKS)):
         replies[c][pl.ds(pl.multiple_of(dp * 8, 8), 8)] = outgoing[c][dp]
 
     loads[1].wait()
@@ -261,11 +260,7 @@
             )
         lat[:, shard, :, at : at + width] = chosen[c][shard]
 
-    def project(c):
-        at, width = CHUNKS[c]
-        for copy in spread[7 * c : 7 * c + 7]:
-            copy.wait_recv()
-
+    def project(at, width):
         @pl.loop(0, CH_DEV)
         def _(n):
             block = lat[pl.ds(2 * n, 2), :, :, at : at + width].reshape(256, width)
@@ -276,9 +271,13 @@
                     for e in range(2):
                         tile = r[:, 128 * e : 128 * e + 128].reshape(16, 16, 128)
                         index = (n >> 1) * 8 + j + e
-                        if c > 0:
+                        if at > 0:
                             tile = tile + total[index, rows]
                         total[index, rows] = tile
+
+    def landed(c):
+        for copy in spread[7 * c : 7 * c + 7]:
+            copy.wait_recv()
 
     arrived(0)
     send_weights(3, down, (dp, up * 2 + core), 0)
@@ -287,11 +286,12 @@
     send_weights(4, up, (dp, down * 2 + core), 1)
     send_weights(6, up, other)
     hand_on(0)
+    hand_on(1)
     arrived(3)
     send_weights(7, far, other, 0)
     arrived(4)
     send_weights(8, far, other, 1)
-    hand_on(1)
+    hand_on(2)
     for kind in (2, 5, 6, 7, 8):
         arrived(kind)
 
@@ -315,13 +315,19 @@
                 jnp.bfloat16
             )
 
-    project(0)
-    hand_on(2)
-    project(1)
-    for b in range(3):
-        turn_latents(b)
-    for copy in spread[14:]:
-        copy.wait_recv()
+    landed(0)
+    project(0, 384)
+    turn_latents(0)
+    hand_on(3)
+    landed(1)
+    turn_latents(1)
+    landed(2)
+    project(384, 256)
+    hand_on(4)
+    landed(3)
+    project(640, 128)
+    turn_latents(2)
+    landed(4)
     turn_latents(3)
 
     eye = one_hot(128, 128, lambda r, c: r == c)
@@ -381,91 +387,74 @@
                 py = flip(py, d % 2 == 0)
         return (pz * 4 + px, py * 2 + core)
 
-    here = place(z * 16 + x * 4 + y, 0)
+    chip = z * 16 + x * 4 + y
     coming = [None] * 16
-    base = [0] * 16
-    root = [0] * 16
 
     def to_other_core(t):
-        coming[t] = send(
-            xs.at[t, 1 - core], crecv.at[t], send_sem.at[0, t], recv_sem.at[0, t], other
-        )
-
-    def totals(k, t):
-        step = min(CHIPS >> (k + 1), 16)
-
-        def summed(at):
+        coming[t] = [
+            send(xs.at[t, 1 - core], crecv.at[t], send_sem.at[0, t], recv_sem.at[0, t], other)
+        ]
+
+    def eight(t, second):
+        code = place(chip, t & 1)
+        high = (t & 1 == 0) != second
+        devices = {}
+        for m in (7, 6, 5, 3, 4, 2, 1):
+            dims = [2 * e + (0 if high else 1) for e in range(3) if m & (4 >> e)]
+            devices[m] = across(dims)
+        return (code & 7 if second else code >> 3), devices
+
+    def exchange_first(t):
+        for copy in coming[t]:
+            copy.wait_recv()
+
+        def summed(at, step):
             where = pl.ds(at, step)
-            if k == 0:
-                return xs[t, core, where].astype(jnp.float32) + crecv[t, where].astype(jnp.float32)
-            back = pl.ds(OFFSETS[k - 1] + at - base[t], step)
-            return acc[t, pl.ds(at - root[t], step)] + rcv[t, back].astype(jnp.float32)
-
-        return summed, step
-
-    def halve(k, t):
-        half = CHIPS >> (k + 1)
-        d = (TURNS[t] + k) % LEVELS
-        bit = (here >> (LEVELS - 1 - d)) & 1
-        away = base[t] + (1 - bit) * half
-        keep = base[t] + bit * half
-        coming[t].wait_recv()
-        if k == 0:
-            root[t] = keep
-        summed, step = totals(k, t)
-
-        @pl.loop(0, half // step)
+            return xs[t, core, where].astype(jnp.float32) + crecv[t, where].astype(jnp.float32)
+
+        @pl.loop(0, 4)
         def _(i):
-            snd[t, pl.ds(OFFSETS[k] + i * step, step)] = summed(away + i * step).astype(
-                jnp.bfloat16
+            snd[t, pl.ds(i * 16, 16)] = summed(i * 16, 16).astype(jnp.bfloat16)
+
+        own, devices = eight(t, False)
+        coming[t] = [
+            send(
+                snd.at[t, pl.ds((own ^ m) * 8, 8)],
+                rcv.at[t, pl.ds(8 * m, 8)],
+                send_sem.at[m, t],
+                recv_sem.at[m, t],
+                device,
             )
-
-        span = pl.ds(OFFSETS[k], half)
-        copy = send(
-            snd.at[t, span],
-            rcv.at[t, span],
-            send_sem.at[1 + k, t],
-            recv_sem.at[1 + k, t],
-            across((d,)),
-        )
-
-        @pl.loop(0, half // step)
-        def _(i):
-            acc[t, pl.ds(keep - root[t] + i * step, step)] = summed(keep + i * step)
-
-        base[t] = keep
-        coming[t] = copy
-
-    last = {}
-
-    def exchange_rest(t):
-        coming[t].wait_recv()
-        whole = acc[t, pl.ds(base[t] - root[t], 8)] + rcv[t, pl.ds(OFFSETS[2], 8)].astype(
-            jnp.float32
-        )
-        acc[t, pl.ds(base[t] - root[t], 8)] = whole
-        snd[t, pl.ds(56, 8)] = whole.astype(jnp.bfloat16)
-        own = place(z * 16 + x * 4 + y, TURNS[t]) & 7
-        last[t] = []
-        for m in (4, 2, 1, 6, 5, 3, 7):
-            dims = [(TURNS[t] + 3 + e) % LEVELS for e in range(3) if m & (4 >> e)]
-            last[t].append(
-                send(
-                    snd.at[t, 56 + (own ^ m)],
-                    rcv.at[t, 56 + m],
-                    send_sem.at[4 + m, t],
-                    recv_sem.at[4 + m, t],
-                    across(dims),
-                )
+            for m, device in devices.items()
+        ]
+        acc[t, pl.ds(0, 8)] = summed(own * 8, 8)
+
+    def exchange_second(t):
+        for copy in coming[t]:
+            copy.wait_recv()
+        whole = acc[t, pl.ds(0, 8)]
+        for m in range(1, 8):
+            whole = whole + rcv[t, pl.ds(8 * m, 8)].astype(jnp.float32)
+        acc[t, pl.ds(0, 8)] = whole
+        snd[t, pl.ds(64, 8)] = whole.astype(jnp.bfloat16)
+        own, devices = eight(t, True)
+        coming[t] = [
+            send(
+                snd.at[t, 64 + (own ^ m)],
+                rcv.at[t, m],
+                send_sem.at[7 + m, t],
+                recv_sem.at[7 + m, t],
+                device,
             )
+            for m, device in devices.items()
+        ]
 
     def finish(t):
-        for copy in last[t]:
+        for copy in coming[t]:
             copy.wait_recv()
-        own = place(z * 16 + x * 4 + y, TURNS[t]) & 7
-        total = acc[t, base[t] - root[t] + own]
+        total = acc[t, place(chip, t & 1) & 7]
         for m in range(1, 8):
-            total = total + rcv[t, 56 + m].astype(jnp.float32)
+            total = total + rcv[t, m].astype(jnp.float32)
         at = 128 * (t % 8)
         grads[16 * (t // 8) : 16 * (t // 8) + 16, at : at + 128] = total
 
@@ -477,7 +466,7 @@
             for j in range(32):
                 for e in range(2):
                     t = 2 * n + e
-                    xs[t, j & 1, place(16 * i + (j >> 1), TURNS[t])] = r[
+                    xs[t, j & 1, place(16 * i + (j >> 1), t & 1)] = r[
                         16 * j : 16 * j + 16, 128 * e : 128 * e + 128
                     ]
 
@@ -495,19 +484,15 @@
                 both = both.astype(jnp.bfloat16)
                 for e in range(2):
                     t = 8 + 2 * n + e
-                    xs[t, j & 1, place(32 * b + (j >> 1), TURNS[t])] = both[
+                    xs[t, j & 1, place(32 * b + (j >> 1), t & 1)] = both[
                         :, 128 * e : 128 * e + 128
                     ]
 
         to_other_core(8 + 2 * n)
         to_other_core(9 + 2 * n)
 
-    def reduce(k, n):
-        for t in (2 * n, 2 * n + 1, 8 + 2 * n, 9 + 2 * n):
-            if k < 3:
-                halve(k, t)
-            else:
-                exchange_rest(t)
+    def parts(n):
+        return (2 * n, 2 * n + 1, 8 + 2 * n, 9 + 2 * n)
 
     for n in range(4):
         attend(256 * n)
@@ -515,13 +500,18 @@
             ctx_copy = pltpu.make_async_copy(ctx, ctx_out, local_sem.at[8])
             ctx_copy.start()
         if n > 0:
-            reduce(0, n - 1)
+            for t in parts(n - 1):
+                exchange_first(t)
         query_sums(n)
         latent_sums(n)
-        for k in range(1, n):
-            reduce(k, n - 1 - k)
-    for k, n in ((0, 3), (1, 2), (2, 1), (3, 0), (1, 3), (2, 2), (3, 1), (2, 3), (3, 2), (3, 3)):
-        reduce(k, n)
+        if n > 1:
+            for t in parts(n - 2):
+                exchange_second(t)
+    for t in parts(3):
+        exchange_first(t)
+    for n in (2, 3):
+        for t in parts(n):
+            exchange_second(t)
     for t in range(16):
         finish(t)
     ctx_copy.wait()
@@ -580,7 +570,7 @@
             pltpu.VMEM((16, 2, CHIPS, 16, 128), bf),
             pltpu.VMEM((16, CHIPS, 16, 128), bf),
             pltpu.VMEM((16, CHIPS // 2, 16, 128), f32),
-            pltpu.VMEM((16, CHIPS, 16, 128), bf),
+            pltpu.VMEM((16, CHIPS + 8, 16, 128), bf),
             pltpu.VMEM((16, CHIPS, 16, 128), bf),
             pltpu.VMEM((16, CHIPS // 2, 16, 128), f32),
             dma((9,)),
@@ -590,12 +580,12 @@
             dma((16,)),
             dma((9, 3)),
             dma((9, 3)),
-            dma((3, 16)),
-            dma((3, 16)),
-            dma((3, 8)),
-            dma((3, 8)),
-            dma((12, 16)),
-            dma((12, 16)),
+            dma((5, 16)),
+            dma((5, 16)),
+            dma((5, 8)),
+            dma((5, 8)),
+            dma((15, 16)),
+            dma((15, 16)),
         ],
         compiler_params=pltpu.CompilerParams(
             collective_id=1, has_side_effects=True, vmem_limit_bytes=67043328

time: 128 us -> 126 us (0.984)
  Pallas kernels: 127 us -> 125 us
    pallas_call x1, Pallas kernels: 125 us -> 123 us  [body(): pl.pallas_call(whole_kernel, out_shape=(jax.ShapeDtypeStruct((256, INNER)...]
where the time goes in v5:
time: 126 us
  Pallas kernels  125 us (99%)
    pallas_call x1, Pallas kernels, body(): pl.pallas_call(whole_kernel, out_shape=(jax.ShapeDtypeStruct((256, INNER)...  123 us

profile of v5, /device:TPU:0, one launch (start us, length us, event | category | flops | bytes accessed | tf_op | source)
XLA Modules:
  0.0 125.5 jit_solution(9879977414154358351)
XLA Ops:
  0.6 123.0 %retro.1 = (bf16[256,1024]{1,0:T(8,128)(2,1)}, f32[32,1024]{1,0:T(8,128)}) custom-call(s32[2,4]{1,0:T(2,128)} %bitcast.1, bf16[256,2048]{1,0:T(8,128)(2,1)} %tok_in.1, bf16[256,1024]{1,0:T(8,128)(2,1)} %cot_in.1, bf16[128,16,896]{2,1,0:T(8,128)(2,1)} %cache_in.1, bf16[256,1024]{1,0:T(8,128)(2,1)} %wq_in.1, bf16[112,1024]{1,0:T(8,128)(2,1)} %wk_in.1, ...), custom_call_target="tpu_custom_call" | custom-call | tf_op jit(solution)/shard_map/retro/pallas_call | solution.py:535
  123.6 1.9 %emit.1 = (bf16[256,1024]{1,0:T(8,128)(2,1)}, f32[16,1024]{1,0:T(8,128)}, f32[7,1024]{1,0:T(8,128)}, f32[7,1024]{1,0:T(8,128)}) custom-call(bf16[256,1024]{1,0:T(8,128)(2,1)} %get-tuple-element.6.ctx, f32[32,1024]{1,0:T(8,128)} %get-tuple-element.7.grads), custom_call_target="tpu_custom_call" | custom-call | tf_op jit(solution)/shard_map/emit/pallas_call | solution.py:603

commit v6 on v5

--- a/solution.py
+++ b/solution.py
@@ -65,14 +65,14 @@
 
 
 def whole_kernel(
-    own_ids, tok_in, cot_in, cache_in, wq_in, wk_in, wv_in, ctx_out, grads, *scratch
+    ids_in, tok_in, cot_in, cache_in, wq_in, wk_in, wv_in, ctx_out, grads, *scratch
 ):
     it = iter(scratch)
 
     def take(n=None):
         return next(it) if n is None else tuple(next(it) for _ in range(n))
 
-    id_row, ids_shard, id_group, ids_dp, asked_v, slots_v, asked_s, slots_s = take(8)
+    own_ids, id_row, ids_shard, id_group, ids_dp, asked_v, slots_v, asked_s, slots_s = take(9)
     cache, tok, cot = take(3)
     weights = take(3)
     wq, wk, wv = weights
@@ -80,14 +80,13 @@
     lat = take()
     normed, normed_t, q, qg, kg, vg, lat_t, ctx = take(8)
     xs, crecv, acc, snd, rcv, value_part = take(6)
-    local_sem, id_send, id_recv, gid_send, gid_recv, w_send, w_recv = take(7)
-    dp_send, dp_recv, sh_send, sh_recv, send_sem, recv_sem = take(6)
+    local_sem, id_sem, w_send, w_recv, dp_send, dp_recv, sh_send, sh_recv = take(8)
+    send_sem, core_recv, first_recv, second_recv = take(4)
 
     dp = lax.axis_index("dp")
     shard = lax.axis_index("shard")
     z, x, y, core = dp // 4, dp % 4, shard // 2, shard % 2
     other = (dp, y * 2 + (1 - core))
-    pending = []
 
     def send(src, dst, ss, rs, device):
         copy = pltpu.make_async_remote_copy(
@@ -99,8 +98,20 @@
             device_id_type=MESH,
         )
         copy.start()
-        pending.append(copy)
-        return copy
+
+    def all_of(ref, sem, sent=False):
+        copy = pltpu.make_async_remote_copy(
+            src_ref=ref,
+            dst_ref=ref,
+            send_sem=sem,
+            recv_sem=sem,
+            device_id=other,
+            device_id_type=MESH,
+        )
+        if sent:
+            copy.wait_send()
+        else:
+            copy.wait_recv()
 
     barrier = pltpu.get_barrier_semaphore()
     for r in range(1, 8):
@@ -113,6 +124,8 @@
         at = pl.multiple_of((row * 2 + side) * n + start, 16)
         return weights[a].at[pl.ds(at, n if size is None else size)]
 
+    ids_copy = pltpu.make_async_copy(ids_in, own_ids, local_sem.at[9])
+    ids_copy.start()
     own_weights = []
     for a, src in enumerate((wq_in, wk_in, wv_in)):
         copy = pltpu.make_async_copy(src, w_rows(a, y, core), local_sem.at[a])
@@ -124,6 +137,7 @@
         copy.start()
         loads.append(copy)
 
+    ids_copy.wait()
     pl.semaphore_wait(barrier, 22)
 
     row_lane = lax.broadcasted_iota(jnp.int32, (8, 128), 1)
@@ -132,39 +146,31 @@
         own_row = jnp.where(row_lane == shard * 8 + k, own_ids[k % 2, k // 2], own_row)
     id_row[...] = own_row
     ids_shard[shard] = own_row
-    asks = [
-        send(id_row, ids_shard.at[shard], id_send.at[r], id_recv.at[r], (dp, shard ^ r))
-        for r in range(1, 8)
-    ]
-    for copy in asks:
-        copy.wait_recv()
+    for r in range(1, 8):
+        send(id_row, ids_shard.at[shard], id_sem.at[0], id_sem.at[1], (dp, shard ^ r))
+    all_of(ids_shard.at[0:7], id_sem.at[1])
     group = ids_shard[0]
     for s in range(1, 8):
         group = group + ids_shard[s]
     id_group[...] = group
     ids_dp[dp] = group
-    asks = [
-        send(id_group, ids_dp.at[dp], gid_send.at[r], gid_recv.at[r], (dp ^ r, shard))
-        for r in DP_ORDER
-    ]
+    for r in DP_ORDER:
+        send(id_group, ids_dp.at[dp], id_sem.at[2], id_sem.at[3], (dp ^ r, shard))
 
     up, down, far = (y + 1) % 4, (y + 3) % 4, (y + 2) % 4
     for copy in own_weights:
         copy.wait()
-    kinds = {}
+    ring = {0: 0, 1: 1, 3: 2, 4: 3}
 
     def send_weights(kind, row, device, part=None):
-        copies = []
         for a in range(3):
             n, cut = WEIGHT_ROWS[a], WEIGHT_CUTS[a]
             start, size = ((0, n), (0, cut), (cut, n - cut))[0 if part is None else 1 + part]
             ref = w_rows(a, row, core, start, size)
-            copies.append(send(ref, ref, w_send.at[kind, a], w_recv.at[kind, a], device))
-        kinds[kind] = copies
+            send(ref, ref, w_send.at[kind // 4 % 2], w_recv.at[ring.get(kind, 4)], device)
 
     def arrived(kind):
-        for copy in kinds[kind]:
-            copy.wait_recv()
+        all_of(wq.at[0:480] if kind < 2 else wq.at[0:240], w_recv.at[ring[kind]])
 
     send_weights(0, y, (dp, up * 2 + core))
     send_weights(1, y, (dp, down * 2 + core))
@@ -179,8 +185,7 @@
         slots = slots + places[o : o + 1]
     slots_v[...] = jnp.broadcast_to(slots, (8, 128))
 
-    for copy in asks:
-        copy.wait_recv()
+    all_of(ids_dp.at[0:15], id_sem.at[3])
     ids = jnp.concatenate([ids_dp[g][0:1] for g in range(16)], axis=0)
     wanted = jnp.where((lane < 64) & ((ids >> 7) == dp), 1, 0)
     asked_v[...] = packed_left(wanted, ids & 127, lane)
@@ -201,21 +206,12 @@
             for c, (at, width) in enumerate(CHUNKS):
                 outgoing[c][g, j] = cache[row, :, at : at + width]
 
-    fetches = []
     for c in range(len(CHUNKS)):
         own = pl.ds(pl.multiple_of(dp * 8, 8), 8)
-        fetches.append(
-            [
-                send(
-                    outgoing[c].at[dp ^ r],
-                    replies[c].at[own],
-                    dp_send.at[c, r],
-                    dp_recv.at[c, r],
-                    (dp ^ r, shard),
-                )
-                for r in DP_ORDER
-            ]
-        )
+        for r in DP_ORDER:
+            send(
+                outgoing[c].at[dp ^ r], replies[c].at[own], dp_send, dp_recv.at[c], (dp ^ r, shard)
+            )
     for c in range(len(CHUNKS)):
         replies[c][pl.ds(pl.multiple_of(dp * 8, 8), 8)] = outgoing[c][dp]
 
@@ -236,12 +232,9 @@
         cols = pl.ds(pl.multiple_of(i * 256, 256), 256)
         normed_t[cols, :] = nt_dot(eye_wide, normed[:, cols]).astype(jnp.bfloat16)
 
-    spread = []
-
     def hand_on(c):
         at, width = CHUNKS[c]
-        for copy in fetches[c]:
-            copy.wait_recv()
+        all_of(replies[c].at[0:120], dp_recv.at[c])
 
         @pl.loop(0, 8)
         def _(s):
@@ -249,14 +242,12 @@
                 chosen[c][s, i] = replies[c][slots_s[0, s * 8 + i]]
 
         for r in range(1, 8):
-            spread.append(
-                send(
-                    chosen[c].at[shard ^ r],
-                    lat.at[:, shard, :, pl.ds(at, width)],
-                    sh_send.at[c, r],
-                    sh_recv.at[c, r],
-                    (dp, shard ^ r),
-                )
+            send(
+                chosen[c].at[shard ^ r],
+                lat.at[:, shard, :, pl.ds(at, width)],
+                sh_send,
+                sh_recv.at[c],
+                (dp, shard ^ r),
             )
         lat[:, shard, :, at : at + width] = chosen[c][shard]
 
@@ -276,8 +267,7 @@
                         total[index, rows] = tile
 
     def landed(c):
-        for copy in spread[7 * c : 7 * c + 7]:
-            copy.wait_recv()
+        all_of(replies[c].at[0:56], sh_recv.at[c])
 
     arrived(0)
     send_weights(3, down, (dp, up * 2 + core), 0)
@@ -292,8 +282,7 @@
     arrived(4)
     send_weights(8, far, other, 1)
     hand_on(2)
-    for kind in (2, 5, 6, 7, 8):
-        arrived(kind)
+    all_of(wq.at[0:1920], w_recv.at[4])
 
     scale = HEAD_DIM ** (-0.5)
 
@@ -388,12 +377,9 @@
         return (pz * 4 + px, py * 2 + core)
 
     chip = z * 16 + x * 4 + y
-    coming = [None] * 16
 
     def to_other_core(t):
-        coming[t] = [
-            send(xs.at[t, 1 - core], crecv.at[t], send_sem.at[0, t], recv_sem.at[0, t], other)
-        ]
+        send(xs.at[t, 1 - core], crecv.at[t], send_sem.at[0], core_recv.at[t // 2], other)
 
     def eight(t, second):
         code = place(chip, t & 1)
@@ -405,8 +391,8 @@
         return (code & 7 if second else code >> 3), devices
 
     def exchange_first(t):
-        for copy in coming[t]:
-            copy.wait_recv()
+        if t % 2 == 0:
+            all_of(crecv.at[0:2], core_recv.at[t // 2])
 
         def summed(at, step):
             where = pl.ds(at, step)
@@ -417,41 +403,36 @@
             snd[t, pl.ds(i * 16, 16)] = summed(i * 16, 16).astype(jnp.bfloat16)
 
         own, devices = eight(t, False)
-        coming[t] = [
+        for m, device in devices.items():
             send(
                 snd.at[t, pl.ds((own ^ m) * 8, 8)],
                 rcv.at[t, pl.ds(8 * m, 8)],
-                send_sem.at[m, t],
-                recv_sem.at[m, t],
+                send_sem.at[1],
+                first_recv.at[t],
                 device,
             )
-            for m, device in devices.items()
-        ]
         acc[t, pl.ds(0, 8)] = summed(own * 8, 8)
 
     def exchange_second(t):
-        for copy in coming[t]:
-            copy.wait_recv()
+        all_of(rcv.at[t, 8:64], first_recv.at[t])
         whole = acc[t, pl.ds(0, 8)]
         for m in range(1, 8):
             whole = whole + rcv[t, pl.ds(8 * m, 8)].astype(jnp.float32)
         acc[t, pl.ds(0, 8)] = whole
         snd[t, pl.ds(64, 8)] = whole.astype(jnp.bfloat16)
         own, devices = eight(t, True)
-        coming[t] = [
+        for m, device in devices.items():
             send(
                 snd.at[t, 64 + (own ^ m)],
                 rcv.at[t, m],
-                send_sem.at[7 + m, t],
-                recv_sem.at[7 + m, t],
+                send_sem.at[2],
+                second_recv.at[t // 2],
                 device,
             )
-            for m, device in devices.items()
-        ]
 
     def finish(t):
-        for copy in coming[t]:
-            copy.wait_recv()
+        if t % 2 == 0:
+            all_of(rcv.at[0:2, 1:8], second_recv.at[t // 2])
         total = acc[t, place(chip, t & 1) & 7]
         for m in range(1, 8):
             total = total + rcv[t, m].astype(jnp.float32)
@@ -515,8 +496,18 @@
     for t in range(16):
         finish(t)
     ctx_copy.wait()
-    for copy in pending:
-        copy.wait_send()
+    for ref, sem in (
+        (ids_shard.at[0:7], id_sem.at[0]),
+        (ids_dp.at[0:15], id_sem.at[2]),
+        (wq.at[0:1920], w_send.at[0]),
+        (wq.at[0:1440], w_send.at[1]),
+        (cache.at[0:120], dp_send),
+        (cache.at[0:56], sh_send),
+        (crecv, send_sem.at[0]),
+        (snd.at[:, 0:56], send_sem.at[1]),
+        (snd.at[:, 0:7], send_sem.at[2]),
+    ):
+        all_of(ref, sem, sent=True)
 
 
 def emit_kernel(ctx, grads, ctx_out, gq, gk, gv):
@@ -538,9 +529,10 @@
             jax.ShapeDtypeStruct((256, INNER), bf),
             jax.ShapeDtypeStruct((32, INNER), f32),
         ),
-        in_specs=[pl.BlockSpec(memory_space=pltpu.SMEM)] + [hbm] * 6,
+        in_specs=[hbm] * 7,
         out_specs=(hbm, vmem),
         scratch_shapes=[
+            pltpu.SMEM((2, 4), i32),
             pltpu.VMEM((8, 128), i32),
             pltpu.VMEM((8, 8, 128), i32),
             pltpu.VMEM((8, 128), i32),
@@ -573,19 +565,18 @@
             pltpu.VMEM((16, CHIPS + 8, 16, 128), bf),
             pltpu.VMEM((16, CHIPS, 16, 128), bf),
             pltpu.VMEM((16, CHIPS // 2, 16, 128), f32),
-            dma((9,)),
-            dma((8,)),
+            dma((10,)),
+            dma((4,)),
+            dma((2,)),
+            dma((5,)),
+            dma,
+            dma((5,)),
+            dma,
+            dma((5,)),
+            dma((3,)),
             dma((8,)),
             dma((16,)),
-            dma((16,)),
-            dma((9, 3)),
-            dma((9, 3)),
-            dma((5, 16)),
-            dma((5, 16)),
-            dma((5, 8)),
-            dma((5, 8)),
-            dma((15, 16)),
-            dma((15, 16)),
+            dma((8,)),
         ],
         compiler_params=pltpu.CompilerParams(
             collective_id=1, has_side_effects=True, vmem_limit_bytes=67043328

time: 126 us -> 117 us (0.929)
  Pallas kernels: 125 us -> 117 us
    pallas_call x1, Pallas kernels: 123 us -> 115 us  [body(): pl.pallas_call(whole_kernel, out_shape=(jax.ShapeDtypeStruct((256, INNER)...]
where the time goes in v6:
time: 117 us
  Pallas kernels  117 us (100%)
    pallas_call x1, Pallas kernels, body(): pl.pallas_call(whole_kernel, out_shape=(jax.ShapeDtypeStruct((256, INNER)...  115 us

profile of v6, /device:TPU:0, one launch (start us, length us, event | category | flops | bytes accessed | tf_op | source)
XLA Modules:
  0.0 117.3 jit_solution(15082986088577119228)
XLA Ops:
  0.6 114.7 %retro.1 = (bf16[256,1024]{1,0:T(8,128)(2,1)}, f32[32,1024]{1,0:T(8,128)}) custom-call(s32[2,4]{1,0:T(2,128)} %bitcast.1, bf16[256,2048]{1,0:T(8,128)(2,1)} %tok_in.1, bf16[256,1024]{1,0:T(8,128)(2,1)} %cot_in.1, bf16[128,16,896]{2,1,0:T(8,128)(2,1)} %cache_in.1, bf16[256,1024]{1,0:T(8,128)(2,1)} %wq_in.1, bf16[112,1024]{1,0:T(8,128)(2,1)} %wk_in.1, ...), custom_call_target="tpu_custom_call" | custom-call | tf_op jit(solution)/shard_map/retro/pallas_call | solution.py:526
  115.4 1.9 %emit.1 = (bf16[256,1024]{1,0:T(8,128)(2,1)}, f32[16,1024]{1,0:T(8,128)}, f32[7,1024]{1,0:T(8,128)}, f32[7,1024]{1,0:T(8,128)}) custom-call(bf16[256,1024]{1,0:T(8,128)(2,1)} %get-tuple-element.6.ctx, f32[32,1024]{1,0:T(8,128)} %get-tuple-element.7.grads), custom_call_target="tpu_custom_call" | custom-call | tf_op jit(solution)/shard_map/emit/pallas_call | solution.py:594

commit v7 on v6

--- a/solution.py
+++ b/solution.py
@@ -310,9 +310,9 @@
     hand_on(3)
     landed(1)
     turn_latents(1)
+    hand_on(4)
     landed(2)
     project(384, 256)
-    hand_on(4)
     landed(3)
     project(640, 128)
     turn_latents(2)
@@ -444,10 +444,11 @@
         def _(i):
             turned = normed_t[pl.ds(pl.multiple_of(i * 512, 512), 512), :]
             r = nn_dot(turned, qg[...]).astype(jnp.bfloat16)
+            start = [place(16 * i, e) for e in range(2)]
             for j in range(32):
                 for e in range(2):
                     t = 2 * n + e
-                    xs[t, j & 1, place(16 * i + (j >> 1), t & 1)] = r[
+                    xs[t, j & 1, start[e] ^ place(j >> 1, e)] = r[
                         16 * j : 16 * j + 16, 128 * e : 128 * e + 128
                     ]
 
@@ -460,12 +461,13 @@
             turned = lat_t[pl.ds(pl.multiple_of(b * 512, 512), 512), :]
             rk = nn_dot(turned, kg[...])
             rv = nn_dot(turned, vg[...])
+            start = [place(32 * b, e) for e in range(2)]
             for j in range(64):
                 both = jnp.concatenate([rk[8 * j : 8 * j + 8], rv[8 * j : 8 * j + 8]], axis=0)
                 both = both.astype(jnp.bfloat16)
                 for e in range(2):
                     t = 8 + 2 * n + e
-                    xs[t, j & 1, place(32 * b + (j >> 1), t & 1)] = both[
+                    xs[t, j & 1, start[e] ^ place(j >> 1, e)] = both[
                         :, 128 * e : 128 * e + 128
                     ]
 
@@ -485,12 +487,12 @@
                 exchange_first(t)
         query_sums(n)
         latent_sums(n)
-        if n > 1:
-            for t in parts(n - 2):
+        if n == 2:
+            for t in parts(0):
                 exchange_second(t)
     for t in parts(3):
         exchange_first(t)
-    for n in (2, 3):
+    for n in (1, 2, 3):
         for t in parts(n):
             exchange_second(t)
     for t in range(16):

time: 117 us -> 115 us (0.983)
  Pallas kernels: 117 us -> 115 us
    pallas_call x1, Pallas kernels: 115 us -> 113 us  [body(): pl.pallas_call(whole_kernel, out_shape=(jax.ShapeDtypeStruct((256, INNER)...]
where the time goes in v7:
time: 115 us
  Pallas kernels  115 us (100%)
    pallas_call x1, Pallas kernels, body(): pl.pallas_call(whole_kernel, out_shape=(jax.ShapeDtypeStruct((256, INNER)...  113 us

profile of v7, /device:TPU:0, one launch (start us, length us, event | category | flops | bytes accessed | tf_op | source)
XLA Modules:
  0.0 115.2 jit_solution(1102599365315402434)
XLA Ops:
  0.6 112.7 %retro.1 = (bf16[256,1024]{1,0:T(8,128)(2,1)}, f32[32,1024]{1,0:T(8,128)}) custom-call(s32[2,4]{1,0:T(2,128)} %bitcast.1, bf16[256,2048]{1,0:T(8,128)(2,1)} %tok_in.1, bf16[256,1024]{1,0:T(8,128)(2,1)} %cot_in.1, bf16[128,16,896]{2,1,0:T(8,128)(2,1)} %cache_in.1, bf16[256,1024]{1,0:T(8,128)(2,1)} %wq_in.1, bf16[112,1024]{1,0:T(8,128)(2,1)} %wk_in.1, ...), custom_call_target="tpu_custom_call" | custom-call | tf_op jit(solution)/shard_map/retro/pallas_call | solution.py:528
  113.3 1.9 %emit.1 = (bf16[256,1024]{1,0:T(8,128)(2,1)}, f32[16,1024]{1,0:T(8,128)}, f32[7,1024]{1,0:T(8,128)}, f32[7,1024]{1,0:T(8,128)}) custom-call(bf16[256,1024]{1,0:T(8,128)(2,1)} %get-tuple-element.6.ctx, f32[32,1024]{1,0:T(8,128)} %get-tuple-element.7.grads), custom_call_target="tpu_custom_call" | custom-call | tf_op jit(solution)/shard_map/emit/pallas_call | solution.py:596

commit v8 on v7

--- a/solution.py
+++ b/solution.py
@@ -456,9 +456,8 @@
         to_other_core(2 * n + 1)
 
     def latent_sums(n):
-        @pl.loop(0, 2)
-        def _(b):
-            turned = lat_t[pl.ds(pl.multiple_of(b * 512, 512), 512), :]
+        for b in range(2):
+            turned = lat_t[512 * b : 512 * b + 512, :]
             rk = nn_dot(turned, kg[...])
             rv = nn_dot(turned, vg[...])
             start = [place(32 * b, e) for e in range(2)]

time: 115 us -> 115 us (level)
  no operation moved by 1% of the time
where the time goes in v8:
time: 115 us
  Pallas kernels  114 us (99%)
    pallas_call x1, Pallas kernels, body(): pl.pallas_call(whole_kernel, out_shape=(jax.ShapeDtypeStruct((256, INNER)...  112 us

profile of v8, /device:TPU:0, one launch (start us, length us, event | category | flops | bytes accessed | tf_op | source)
XLA Modules:
  0.0 114.8 jit_solution(18326779219529227228)
XLA Ops:
  0.6 112.2 %retro.1 = (bf16[256,1024]{1,0:T(8,128)(2,1)}, f32[32,1024]{1,0:T(8,128)}) custom-call(s32[2,4]{1,0:T(2,128)} %bitcast.1, bf16[256,2048]{1,0:T(8,128)(2,1)} %tok_in.1, bf16[256,1024]{1,0:T(8,128)(2,1)} %cot_in.1, bf16[128,16,896]{2,1,0:T(8,128)(2,1)} %cache_in.1, bf16[256,1024]{1,0:T(8,128)(2,1)} %wq_in.1, bf16[112,1024]{1,0:T(8,128)(2,1)} %wk_in.1, ...), custom_call_target="tpu_custom_call" | custom-call | tf_op jit(solution)/shard_map/retro/pallas_call | solution.py:527
  112.9 1.9 %emit.1 = (bf16[256,1024]{1,0:T(8,128)(2,1)}, f32[16,1024]{1,0:T(8,128)}, f32[7,1024]{1,0:T(8,128)}, f32[7,1024]{1,0:T(8,128)}) custom-call(bf16[256,1024]{1,0:T(8,128)(2,1)} %get-tuple-element.6.ctx, f32[32,1024]{1,0:T(8,128)} %get-tuple-element.7.grads), custom_call_target="tpu_custom_call" | custom-call | tf_op jit(solution)/shard_map/emit/pallas_call | solution.py:595
